TPU v7x, 32 devices: a whole 2x2x4 slice. The times are simulated.
32 devices in a mesh: lat: 4 (over z), dom: 2 (over y), ens: 4 (over x, core).
Axes of the slice: x: 2, y: 2, z: 4, core: 2. Of those that a mesh axis runs over, the one named last changes fastest.
Arguments:
- ens_state: bfloat16 [256, 32, 1024, 32], P('ens', 'lat', 'dom')
- w_in: bfloat16 [64, 128], replicated
- w_out: bfloat16 [128, 32], replicated
- obs_op: bfloat16 [32, 16], replicated
- obs_val: float32 [32, 4, 256, 16], P('lat', 'dom')
- obs_wt: float32 [32, 4, 256, 16], P('lat', 'dom')
Outputs:
- output: bfloat16 [256, 32, 1024, 32], P('ens', 'lat', 'dom')
All inputs are finite; a program needn't handle non-finite values.
Results may differ from a plain program's by a relative error of at most 0.001.
Values are sent between devices in bfloat16 or wider.
A program may use at most 1 GiB of HBM per device.

v0:
```python
import math
import jax
import jax.numpy as jnp
from jax import lax
from jax.sharding import PartitionSpec as P

NS_STEPS = 12
TOP_PRECISION = lax.Precision.HIGHEST


def value_a14(block, w_in, w_out, lat_count, dom_count):
    chan_count = block.shape[-1]
    lat_index = lax.axis_index('lat')
    to_next = [(source, source + 1) for source in range(lat_count - 1)]
    to_prev = [(source + 1, source) for source in range(lat_count - 1)]
    east_perm = [(source, (source + 1) % dom_count) for source in range(dom_count)]
    west_perm = [(source, (source - 1) % dom_count) for source in range(dom_count)]
    from_above = lax.ppermute(block[:, -1:], 'lat', to_next)
    from_below = lax.ppermute(block[:, :1], 'lat', to_prev)
    from_west = lax.ppermute(block[:, :, -1:], 'dom', east_perm)
    from_east = lax.ppermute(block[:, :, :1], 'dom', west_perm)
    halo_above = jnp.where(lat_index == 0, block[:, :1], from_above)
    halo_below = jnp.where(lat_index == lat_count - 1, block[:, -1:], from_below)
    x_f32 = block.astype(jnp.float32)
    row_above = jnp.concatenate([halo_above, block[:, :-1]], axis=1).astype(jnp.float32)
    row_below = jnp.concatenate([block[:, 1:], halo_below], axis=1).astype(jnp.float32)
    col_west = jnp.concatenate([from_west, block[:, :, :-1]], axis=2).astype(jnp.float32)
    col_east = jnp.concatenate([block[:, :, 1:], from_east], axis=2).astype(jnp.float32)
    laplace = (row_above + row_below + col_west + col_east - 4.0 * x_f32).astype(jnp.bfloat16)
    pre_act = jnp.einsum('mrwc,ch->mrwh', block, w_in[:chan_count], preferred_element_type=jnp.float32)
    pre_act = pre_act + jnp.einsum('mrwc,ch->mrwh', laplace, w_in[chan_count:], preferred_element_type=jnp.float32)
    hidden = jax.nn.gelu(pre_act, approximate=False).astype(jnp.bfloat16)
    update = jnp.einsum('mrwh,hc->mrwc', hidden, w_out, preferred_element_type=jnp.float32)
    return (x_f32 + update).astype(jnp.bfloat16)


def analyse_block(xf_block, obs_vals, obs_wts, obs_op):
    member_count, row_count, col_count, chan_count = xf_block.shape
    patch_count, patch_len, obs_count = obs_vals.shape[1:]
    obs_width = patch_len * obs_count
    xf_patch = xf_block.reshape(member_count, row_count, patch_count, patch_len, chan_count)
    x_mean = jnp.mean(xf_patch, axis=0, dtype=jnp.float32)
    x_anom = xf_patch.astype(jnp.float32) - x_mean
    y_back = jnp.einsum('ernbc,co->ernbo', xf_patch, obs_op, preferred_element_type=jnp.float32)
    y_mean = jnp.mean(y_back, axis=0)
    y_anom = (y_back - y_mean).reshape(member_count, row_count, patch_count, obs_width)
    c_mat = y_anom * obs_wts.reshape(row_count, patch_count, obs_width)
    eye_mat = jnp.eye(member_count, dtype=jnp.float32)
    a_mat = jnp.einsum('ernq,frnq->rnef', c_mat, y_anom, precision=TOP_PRECISION) + (member_count - 1) * eye_mat
    scale_f = jnp.sqrt(jnp.sum(a_mat * a_mat, axis=(2, 3), keepdims=True))
    y_mat = a_mat / scale_f
    z_mat = jnp.broadcast_to(eye_mat, a_mat.shape)
    for step_index in range(NS_STEPS):
        t_mat = 1.5 * eye_mat - 0.5 * jnp.einsum('rnij,rnjk->rnik', z_mat, y_mat, precision=TOP_PRECISION)
        y_mat = jnp.einsum('rnij,rnjk->rnik', y_mat, t_mat, precision=TOP_PRECISION)
        z_mat = jnp.einsum('rnij,rnjk->rnik', t_mat, z_mat, precision=TOP_PRECISION)
    s_mat = z_mat / jnp.sqrt(scale_f)
    pa_mat = jnp.einsum('rnij,rnjk->rnik', s_mat, s_mat, precision=TOP_PRECISION)
    innovation = obs_vals.reshape(row_count, patch_count, obs_width) - y_mean.reshape(row_count, patch_count, obs_width)
    c_innov = jnp.einsum('ernq,rnq->rne', c_mat, innovation, precision=TOP_PRECISION)
    w_mean = jnp.einsum('rnef,rnf->rne', pa_mat, c_innov, precision=TOP_PRECISION)
    t_mat = math.sqrt(member_count - 1) * s_mat + w_mean[..., None]
    x_anal = x_mean + jnp.einsum('krnbc,rnke->ernbc', x_anom, t_mat, precision=TOP_PRECISION)
    return x_anal.astype(jnp.bfloat16).reshape(member_count, row_count, col_count, chan_count)


def solution(mesh):
    lat_count = mesh.shape['lat']
    dom_count = mesh.shape['dom']

    def local_cycle(ens_block, w_in, w_out, obs_op, obs_val, obs_wt):
        value_a8 = value_a14(ens_block, w_in, w_out, lat_count, dom_count)
        by_point = lax.all_to_all(value_a8, 'ens', 1, 0, tiled=True)
        row_share = by_point.shape[1]
        row_start = lax.axis_index('ens') * row_share
        obs_rows = lax.dynamic_slice_in_dim(obs_val, row_start, row_share, axis=0)
        wt_rows = lax.dynamic_slice_in_dim(obs_wt, row_start, row_share, axis=0)
        analysed = analyse_block(by_point, obs_rows, wt_rows, obs_op)
        return lax.all_to_all(analysed, 'ens', 0, 1, tiled=True)

    state_spec = P('ens', 'lat', 'dom', None)
    obs_spec = P('lat', 'dom', None, None)
    return jax.shard_map(local_cycle, mesh=mesh, in_specs=(state_spec, P(), P(), P(), obs_spec, obs_spec), out_specs=state_spec, check_vma=False)
```

profile of v0, /device:TPU:0, one launch (start us, length us, event | category | flops | bytes accessed | tf_op | source)
XLA Modules:
  0.0 1358.1 jit_solution(14037548223708652520)
XLA Ops:
  32.1 50.6 %fusion.76 = f32[64,8,512,128]{3,2,1,0:T(8,128)} fusion(bf16[64,8,512,32]{2,3,1,0:T(8,128)(2,1)} %param.6, bf16[64,128]{1,0:T(8,128)(2,1)S(1)} %copy-done.2), kind=kOutput, calls=%fused_computation.111 | convolution fusion | flops 2147483648 | bytes 151003136 | tf_op jit(solution)/shard_map/mrwc,ch->mrwh/dot_general | solution.py:30
  82.7 27.6 %fusion.117 = (bf16[64,8,511,32]{2,3,1,0:T(8,128)(2,1)}, bf16[64,8,511,32]{2,3,1,0:T(8,128)(2,1)}) fusion(bf16[64,8,512,32]{2,3,1,0:T(8,128)(2,1)} %param.6), kind=kLoop, calls=%fused_computation.156 | loop fusion | bytes 66977792 | tf_op jit(solution)/shard_map/slice | solution.py:28
  110.3 22.5 %fusion.119 = (bf16[64,7,512,32]{2,3,1,0:T(8,128)(2,1)}, bf16[64,7,512,32]{2,3,1,0:T(8,128)(2,1)}) fusion(bf16[64,8,512,32]{2,3,1,0:T(8,128)(2,1)} %param.6), kind=kLoop, calls=%fused_computation.158 | loop fusion | bytes 58720256 | tf_op jit(solution)/shard_map/slice | solution.py:26
  132.8 7.8 copy.50
  140.5 7.7 copy.52
  151.8 37.8 %fusion.23.clone.5 = bf16[64,8,512,32]{2,3,1,0:T(8,128)(2,1)} fusion(bf16[64,8,512,32]{2,3,1,0:T(8,128)(2,1)} %param.6, bf16[64,7,512,32]{2,3,1,0:T(8,128)(2,1)} %get-tuple-element.12, bf16[64,1,512,32]{2,3,1,0:T(8,128)(2,1)S(1)} %get-tuple-element.14, bf16[64,1,512,32]{2,3,1,0:T(8,128)(2,1)S(1)} %get-tuple-element.13, ...), kind=kLoop, calls=%fused_computation.27.clone.clone.clone.clone.2 | loop fusion | flops 192937984 | bytes 100663296
  189.6 118.3 %fusion.17 = (u8[64,512,128]{2,1,0:T(8,128)(4,1)}, u8[64,512,128]{2,1,0:T(8,128)(4,1)}, f32[64,8,512,128]{3,2,1,0:T(8,128)}) fusion(f32[64,8,512,128]{3,2,1,0:T(8,128)} %fusion.76, bf16[64,128]{1,0:T(8,128)(2,1)S(1)} %copy-done.2, bf16[64,8,512,32]{2,3,1,0:T(8,128)(2,1)} %fusion.23.clone.5), kind=kOutput, calls=%fused_computation.35 | convolution fusion | flops 2608857088 | bytes 293609472 | tf_op jit(solution)/shard_map/mrwc,ch->mrwh/dot_general | solution.py:31
  307.9 322.6 %fusion.13 = bf16[64,8,512,32]{2,3,1,0:T(8,128)(2,1)S(1)} fusion(bf16[64,8,512,32]{2,3,1,0:T(8,128)(2,1)} %param.6, f32[64,8,512,128]{3,2,1,0:T(8,128)} %get-tuple-element.21, u8[64,512,128]{2,1,0:T(8,128)(4,1)} %get-tuple-element.6, u8[64,512,128]{2,1,0:T(8,128)(4,1)} %get-tuple-element.5, bf16[128,32]{0,1:T(8,128)(2,1)S(1)} %copy-done), kind=kOutput, calls=%fused_computation.28 | convolution fusion | flops 4521459712 | bytes 176168960 | tf_op jit(solution)/shard_map/mrwh,hc->mrwc/dot_general | solution.py:33
  630.5 7.1 copy.53
  637.6 7.0 all-to-all-start
  644.7 182.6 %all-to-all-done = bf16[64,8,512,32]{2,3,0,1:T(8,128)(2,1)} async-done(((bf16[64,8,512,32]{2,3,0,1:T(8,128)(2,1)}), bf16[64,8,512,32]{2,3,0,1:T(8,128)(2,1)}, u32[]{:S(2)}, u32[]{:S(2)}) %all-to-all-start) | async-done | bytes 16777248 | tf_op jit(solution)/shard_map/all_to_all | solution.py:73
  827.3 14.2 %copy_bitcast_fusion = bf16[4,64,2,512,32]{3,4,2,1,0:T(8,128)(2,1)} fusion(bf16[64,8,512,32]{2,3,0,1:T(8,128)(2,1)} %all-to-all-done), kind=kLoop, calls=%fused_computation.57 | loop fusion | bytes 33554432 | tf_op jit(solution)/shard_map/all_to_all | solution.py:73
  841.4 23.7 %reshape.51 = bf16[256,2,2,256,32]{3,2,4,1,0:T(2,128)(2,1)} reshape(bf16[4,64,2,512,32]{3,4,2,1,0:T(8,128)(2,1)} %copy_bitcast_fusion) | data formatting | bytes 33554432 | tf_op jit(solution)/shard_map/reshape | solution.py:41
  865.2 11.8 fusion.121
  877.9 12.1 broadcast_subtract_fusion
  890.0 20.2 %copy.57 = f32[256,2,2,256,16]{0,4,3,2,1:T(8,128)} copy(f32[256,2,2,256,16]{3,4,2,1,0:T(8,128)} %broadcast_subtract_fusion) | data formatting | bytes 33554432 | tf_op jit(solution)/shard_map/sub | solution.py:46
  910.7 40.3 %multiply_reduce_fusion = (f32[2,2]{1,0:T(2,128)S(1)}, f32[2,2,256,256]{3,2,1,0:T(8,128)S(1)}) fusion(f32[256,256]{1,0:T(8,128)S(1)} %fusion.71, f32[256,2,2,4096]{0,3,2,1:T(8,128)} %bitcast.153, f32[2,2,4096]{2,1,0:T(2,128)S(1)} %mul.130), kind=kOutput, calls=%fused_computation.93 | convolution fusion | flops 12889882624 | bytes 18153488 | tf_op jit(solution)/shard_map/ernq,frnq->rnef/dot_general | solution.py:49
  990.8 12.1 fusion.18
  1014.8 19.1 %convert_subtract_fusion = f32[256,2,8,256,8]{3,2,4,1,0:T(8,128)} fusion(bf16[256,2,8,256,8]{3,2,4,1,0:T(8,128)(2,1)} %bitcast.156, f32[2,8,256,8]{2,1,3,0:T(8,128)S(1)} %bitcast.161), kind=kLoop, calls=%fused_computation.32 | loop fusion | flops 16777216 | bytes 50462720 | tf_op jit(solution)/shard_map/sub | solution.py:43
  1033.8 80.7 %fusion.22 = bf16[256,2,2,256,32]{0,3,4,2,1:T(8,128)(2,1)} fusion(f32[2,2,256,32]{2,3,1,0:T(8,128)S(1)} %bitcast.159, f32[256,2,2,256,32]{3,2,4,1,0:T(2,128)} %bitcast.155, f32[2,2,256,256,1]{3,2,4,1,0:T(8,128)S(1)} %fusion.226), kind=kOutput, calls=%fused_computation.40 | convolution fusion | flops 25786580992 | bytes 51511296 | tf_op jit(solution)/shard_map/krnbc,rnke->ernbc/dot_general | solution.py:63
  1114.5 17.9 %copy.63 = bf16[256,2,2,256,32]{0,4,3,2,1:T(8,128)(2,1)} copy(bf16[256,2,2,256,32]{0,3,4,2,1:T(8,128)(2,1)} %fusion.22) | data formatting | bytes 33554432 | tf_op jit(solution)/shard_map/convert_element_type | solution.py:64
  1132.5 30.6 %copy.64 = bf16[256,2,512,32]{2,3,1,0:T(8,128)(2,1)} copy(bf16[256,2,512,32]{0,3,2,1:T(8,128)(2,1)} %bitcast.157) | data formatting | bytes 33554432 | tf_op jit(solution)/shard_map/reshape | solution.py:64
  1163.1 187.5 %all_to_all.33 = bf16[256,2,512,32]{2,3,1,0:T(8,128)(2,1)S(1)} all-to-all(bf16[256,2,512,32]{2,3,1,0:T(8,128)(2,1)} %copy.64), channel_id=1, replica_groups=mesh['lat'=4,'dom'=2,'ens'=4] {'ens'}, dimensions={0} | all-to-all | bytes 33554432 | tf_op jit(solution)/shard_map/all_to_all | solution.py:79
  1350.6 7.1 copy.65
  (74 shorter events, 88.4 us)
Async XLA Ops:
  0.0 307.9 %copy-start = (bf16[128,32]{0,1:T(8,128)(2,1)S(1)}, bf16[128,32]{0,1:T(8,128)(2,1)}, u32[]{:S(2)}) copy-start(bf16[128,32]{0,1:T(8,128)(2,1)} %param.8) | copy-start | bytes 24580
  0.0 32.1 %copy-start.2 = (bf16[64,128]{1,0:T(8,128)(2,1)S(1)}, bf16[64,128]{1,0:T(8,128)(2,1)}, u32[]{:S(2)}) copy-start(bf16[64,128]{1,0:T(8,128)(2,1)} %param.7) | copy-start | bytes 49156
  4.8 143.5 %collective-permute-start = (bf16[64,1,512,32]{2,3,1,0:T(8,128)(2,1)}, bf16[64,1,512,32]{2,3,1,0:T(8,128)(2,1)S(1)}, u32[]{:S(2)}, u32[]{:S(2)}) collective-permute-start(bf16[64,1,512,32]{2,3,1,0:T(8,128)(2,1)} %get-tuple-element.16), channel_id=1, source_target_pairs={{0,8},{8,16},{16,24},{1,9},{9,17},{17,25},{2,10},{10,18},{18,26},{... | collective-permute-start | bytes 6291464 | tf_op jit(solution)/shard_map/ppermute | solution.py:18
  9.9 138.4 %collective-permute-start.1 = (bf16[64,1,512,32]{2,3,1,0:T(8,128)(2,1)}, bf16[64,1,512,32]{2,3,1,0:T(8,128)(2,1)}, u32[]{:S(2)}, u32[]{:S(2)}) collective-permute-start(bf16[64,1,512,32]{2,3,1,0:T(8,128)(2,1)} %get-tuple-element.15), channel_id=1, source_target_pairs={{8,0},{16,8},{24,16},{9,1},{17,9},{25,17},{10,2},{18,10},{26,18},{... | collective-permute-start | bytes 6291464 | tf_op jit(solution)/shard_map/ppermute | solution.py:19
  24.0 108.8 %collective-permute-start.2 = (bf16[64,8,1,32]{0,3,2,1:T(8,128)(2,1)S(1)}, bf16[64,8,1,32]{0,3,2,1:T(8,128)(2,1)S(1)}, u32[]{:S(2)}, u32[]{:S(2)}) collective-permute-start(bf16[64,8,1,32]{0,3,2,1:T(8,128)(2,1)S(1)} %copy.77), channel_id=1, source_target_pairs={{0,4},{4,0},{1,5},{5,1},{2,6},{6,2},{3,7},{7,3},{8,12},{12,8},{9,1... | collective-permute-start | bytes 98312 | tf_op jit(solution)/shard_map/ppermute | solution.py:20
  31.6 109.0 %collective-permute-start.3 = (bf16[64,8,1,32]{0,3,2,1:T(8,128)(2,1)S(1)}, bf16[64,8,1,32]{0,3,2,1:T(8,128)(2,1)S(1)}, u32[]{:S(2)}, u32[]{:S(2)}) collective-permute-start(bf16[64,8,1,32]{0,3,2,1:T(8,128)(2,1)S(1)} %copy.78), channel_id=1, source_target_pairs={{0,4},{4,0},{1,5},{5,1},{2,6},{6,2},{3,7},{7,3},{8,12},{12,8},{9,1... | collective-permute-start | bytes 98312 | tf_op jit(solution)/shard_map/ppermute | solution.py:21
  637.6 189.7 %all-to-all-start = ((bf16[64,8,512,32]{2,3,0,1:T(8,128)(2,1)}), bf16[64,8,512,32]{2,3,0,1:T(8,128)(2,1)}, u32[]{:S(2)}, u32[]{:S(2)}) async-start(bf16[64,8,512,32]{2,3,0,1:T(8,128)(2,1)} %copy.53), calls=%async_computation | async-start | bytes 33554432 | tf_op jit(solution)/shard_map/all_to_all | solution.py:73
  644.7 220.5 %copy-start.3 = (bf16[32,16]{0,1:T(8,128)(2,1)S(1)}, bf16[32,16]{0,1:T(8,128)(2,1)}, u32[]{:S(2)}) copy-start(bf16[32,16]{0,1:T(8,128)(2,1)} %param.9) | copy-start | bytes 3076
  1132.5 225.2 %copy-start.1 = (bf16[128,32]{0,1:T(8,128)(2,1)S(1)}, bf16[128,32]{0,1:T(8,128)(2,1)}, u32[]{:S(2)}) copy-start(bf16[128,32]{0,1:T(8,128)(2,1)} %param.8) | copy-start | bytes 24580
where the time goes:
time: 1370 us; the launch traced here: 1360 us
  matrix products  680 us (50%)
  local copies, waits for them, and re-layouts  211 us (15%)
  blocking collectives  187 us (14%)
  waiting for transfers between devices  183 us (13%)
  other arithmetic  80.6 us (6%)
  starting transfers between devices  15.5 us (1%)
    dot_general x1, matrix products, value_a14(): jnp.einsum('mrwh,hc->mrwc', hidden, w_out, preferred_element_type=jnp.flo...  323 us
    all_to_all x1, blocking collectives, local_cycle(): return lax.all_to_all(analysed, 'ens', 0, 1, tiled=True)  187 us
    all_to_all x1, waiting for transfers between devices, local_cycle(): by_point = lax.all_to_all(value_a8, 'ens', 1, 0, tiled=True)  183 us
    dot_general x1, matrix products, value_a14(): jnp.einsum('mrwc,ch->mrwh', laplace, w_in[chan_count:], preferred_element...  118 us
    dot_general x1, matrix products, analyse_block(): jnp.einsum('krnbc,rnke->ernbc', x_anom, t_mat, precision=TOP_PRECISION)  80.7 us
    dot_general x1, matrix products, value_a14(): jnp.einsum('mrwc,ch->mrwh', block, w_in[:chan_count], preferred_element_t...  50.6 us
    dot_general x1, matrix products, analyse_block(): jnp.einsum('ernq,frnq->rnef', c_mat, y_anom, precision=TOP_PRECISION)  40.3 us
    unnamed x1, other arithmetic  37.8 us
  transfers between devices with their start and end apart: 5, of which 1 were waited for; matrix products, arithmetic and copies ran while one was open for 10% of the time, Pallas kernels for 0%

commit v1 on v0

v1 whole, which is shorter than its diff:
```python
import functools
import math

import jax
import jax.numpy as jnp
import numpy as np
from jax import lax
from jax.experimental import pallas as pl
from jax.experimental.pallas import tpu as pltpu
from jax.sharding import PartitionSpec as P

NS_STEPS = 12
MESH = pl.DeviceIdType.MESH
F32 = jnp.float32
BF16 = jnp.bfloat16
MEMBERS = 256
MINE = 64
ROWS = 8
COLS = 512
CHANS = 32
PATCH = 256
OBS = 16
CHUNKS = 4
OWNERS = 4
GROUP = 16
SUBS = MINE // GROUP
STAGE = CHUNKS * OWNERS


def split3(value):
    high = value.astype(BF16)
    rest = value - high.astype(F32)
    mid = rest.astype(BF16)
    low = (rest - mid.astype(F32)).astype(BF16)
    return high, mid, low


def dot(a, b):
    return jnp.dot(a, b, preferred_element_type=F32)


def dot_t(a, b):
    return lax.dot_general(a, b, (((1,), (1,)), ((), ())), preferred_element_type=F32)


def dot6(a, b):
    small = dot(a[2][...], b[0][...]) + dot(a[0][...], b[2][...]) + dot(a[1][...], b[1][...])
    return small + dot(a[1][...], b[0][...]) + dot(a[0][...], b[1][...]) + dot(a[0][...], b[0][...])


def chunk_row(chunk, which):
    last = chunk // (CHUNKS - 1)
    return (1 - last) * (1 + 2 * chunk + which) + last * (ROWS - 1) * which


def kernel(lat_count, dom_count, w1_ref, w2_ref, bd_ref, perm_ref, yo_ref, wt_ref, x_ref, out_ref,
           buf, xbuf, edge_out, edge_in, work, am, pm, zm, cif, sy, sz, st, xbar, ybar, sw_ref, sd_ref,
           x_sem, halo_send, halo_recv, halo_local, edge_send, edge_recv, f_send, f_recv, r_send, r_recv, own_sem):
    me = lax.axis_index('ens')
    lat = lax.axis_index('lat')
    dom = lax.axis_index('dom')
    my_row = me // 2
    my_half = me % 2
    lat_up = (lat + lat_count - 1) % lat_count
    lat_down = (lat + 1) % lat_count
    dom_other = (dom + 1) % dom_count

    row_copies = [pltpu.make_async_copy(x_ref.at[:, r], xbuf.at[r + 1], x_sem.at[r]) for r in range(ROWS)]
    for r in range(ROWS):
        row_copies[r].start()

    barrier = pltpu.get_barrier_semaphore()
    for t in range(1, OWNERS):
        pl.semaphore_signal(barrier, inc=1, device_id={'ens': (me + t) % OWNERS}, device_id_type=MESH)
    pl.semaphore_signal(barrier, inc=1, device_id={'lat': lat_up}, device_id_type=MESH)
    pl.semaphore_signal(barrier, inc=1, device_id={'lat': lat_down}, device_id_type=MESH)
    pl.semaphore_signal(barrier, inc=1, device_id={'dom': dom_other}, device_id_type=MESH)
    pl.semaphore_wait(barrier, OWNERS + 2)

    send_up = pltpu.make_async_remote_copy(x_ref.at[:, 0], xbuf.at[ROWS + 1], halo_send.at[0], halo_recv.at[1],
                                           device_id={'lat': lat_up}, device_id_type=MESH)
    send_down = pltpu.make_async_remote_copy(x_ref.at[:, ROWS - 1], xbuf.at[0], halo_send.at[1], halo_recv.at[0],
                                             device_id={'lat': lat_down}, device_id_type=MESH)
    top_copy = pltpu.make_async_copy(x_ref.at[:, 0], xbuf.at[0], halo_local.at[0])
    bottom_copy = pltpu.make_async_copy(x_ref.at[:, ROWS - 1], xbuf.at[ROWS + 1], halo_local.at[1])

    @pl.when(lat > 0)
    def _():
        send_up.start()

    @pl.when(lat < lat_count - 1)
    def _():
        send_down.start()

    @pl.when(lat == 0)
    def _():
        top_copy.start()

    @pl.when(lat == lat_count - 1)
    def _():
        bottom_copy.start()

    lane = lax.broadcasted_iota(jnp.int32, (CHANS, 128), 1)

    def edge_copy(chunk):
        return pltpu.make_async_remote_copy(edge_out.at[chunk], edge_in.at[chunk], edge_send.at[chunk], edge_recv.at[chunk],
                                            device_id={'dom': dom_other}, device_id_type=MESH)

    def pack(chunk, carry):
        def member(m, acc):
            first, last = acc
            for which in range(2):
                row = chunk_row(chunk, which) + 1
                spot = lane == which * MINE + m
                west = xbuf[row, m, :, 0:128].astype(F32)
                east = xbuf[row, m, :, COLS - 128:COLS].astype(F32)
                first = jnp.where(spot, west[:, 0:1], first)
                last = jnp.where(spot, east[:, 127:128], last)
            return first, last

        zero = jnp.zeros((CHANS, 128), F32)
        first, last = lax.fori_loop(0, MINE, member, (zero, zero))
        edge_out[chunk, 0] = first.astype(BF16)
        edge_out[chunk, 1] = last.astype(BF16)
        edge_copy(chunk).start()
        return carry

    for r in range(4):
        row_copies[r].wait()
    pack(0, 0)
    for r in range(4, ROWS):
        row_copies[r].wait()
    lax.fori_loop(1, CHUNKS, pack, 0)

    def f_copy(chunk, t, start, size):
        owner = (me + t) % OWNERS
        return pltpu.make_async_remote_copy(
            buf.at[STAGE + 3 * chunk + t - 1, pl.ds(start, size)], buf.at[OWNERS * chunk + me, pl.ds(start, size)],
            f_send.at[chunk, t - 1], f_recv.at[chunk, me], device_id={'ens': owner}, device_id_type=MESH)

    def forecast_chunk(chunk, carry):
        edge_copy(chunk).wait_recv()

        @pl.when((chunk == CHUNKS - 1) & (lat > 0))
        def _():
            send_down.wait_recv()

        @pl.when((chunk == CHUNKS - 1) & (lat == 0))
        def _():
            top_copy.wait()

        @pl.when((chunk == CHUNKS - 1) & (lat < lat_count - 1))
        def _():
            send_up.wait_recv()

        @pl.when((chunk == CHUNKS - 1) & (lat == lat_count - 1))
        def _():
            bottom_copy.wait()

        slots = []
        for owner in range(OWNERS):
            ahead = (owner - me + OWNERS) % OWNERS
            own = 1 - (ahead + OWNERS - 1) // OWNERS
            slots.append(own * (OWNERS * chunk + me) + (1 - own) * (STAGE + 3 * chunk + ahead - 1))

        def member(m, carry):
            from_east = edge_in[chunk, 0].astype(F32)
            from_west = edge_in[chunk, 1].astype(F32)
            for which in range(2):
                row = chunk_row(chunk, which) + 1
                spot = which * MINE + m
                halo_west = pltpu.roll(from_west, (128 - spot) % 128, 1)
                halo_east = pltpu.roll(from_east, 127 - spot, 1)
                here = xbuf[row, m]
                mid = here.astype(F32)
                above = xbuf[row - 1, m].astype(F32)
                below = xbuf[row + 1, m].astype(F32)
                west = pltpu.roll(mid, 1, 1)
                east = pltpu.roll(mid, COLS - 1, 1)
                west = jnp.concatenate([jnp.where(lane == 0, halo_west, west[:, :128]), west[:, 128:]], axis=1)
                east = jnp.concatenate([east[:, :COLS - 128], jnp.where(lane == 127, halo_east, east[:, COLS - 128:])], axis=1)
                laplace = (above + below + west + east - 4.0 * mid).astype(BF16)
                for half in range(2):
                    span = slice(half * PATCH, (half + 1) * PATCH)
                    features = jnp.concatenate([here[:, span], laplace[:, span]], axis=0)
                    pre_act = dot(w1_ref[...], features)
                    hidden = (0.5 * pre_act * (1.0 + lax.erf(pre_act * math.sqrt(0.5)))).astype(BF16)
                    update = dot(w2_ref[...], hidden)
                    buf[slots[2 * which + half], m] = (mid[:, span] + update).astype(BF16)
            return carry

        def sub(index, carry):
            start = index * GROUP
            lax.fori_loop(start, start + GROUP, member, 0)
            for t in (2, 1, 3):
                f_copy(chunk, t, start, GROUP).start()
            return carry

        lax.fori_loop(0, SUBS, sub, 0)
        return carry

    lax.fori_loop(0, CHUNKS, forecast_chunk, 0)

    def r_place(chunk, owner):
        return out_ref.at[:, chunk_row(chunk, owner // 2), :, pl.ds(pl.multiple_of((owner % 2) * PATCH, PATCH), PATCH)]

    def r_stage(chunk, target):
        return xbuf.at[2 * chunk + target // 2, :, :, (target % 2) * PATCH:(target % 2 + 1) * PATCH]

    def r_copy(chunk, target):
        return pltpu.make_async_remote_copy(
            r_stage(chunk, target), r_place(chunk, me), r_send.at[chunk, target], r_recv.at[chunk, me],
            device_id={'ens': target}, device_id_type=MESH)

    def own_copy(chunk, target):
        return pltpu.make_async_copy(r_stage(chunk, target), r_place(chunk, me), own_sem.at[chunk])

    row_id = lax.broadcasted_iota(jnp.int32, (MEMBERS, MEMBERS), 0)
    col_id = lax.broadcasted_iota(jnp.int32, (MEMBERS, MEMBERS), 1)

    def analyse(chunk, carry):
        for t in range(1, OWNERS):
            source = (me + t) % OWNERS
            pltpu.make_async_remote_copy(
                buf.at[STAGE], buf.at[OWNERS * chunk + source], f_send.at[chunk, 0], f_recv.at[chunk, source],
                device_id={'ens': source}, device_id_type=MESH).wait_recv()
        row = chunk_row(chunk, my_row)

        def block(group):
            return buf[OWNERS * chunk + group // SUBS, pl.ds((group % SUBS) * GROUP, GROUP)]

        def sums(group, acc):
            x_sum, y_sum = acc
            states = block(group)
            x_sum = x_sum + jnp.sum(states.astype(F32), axis=0)
            for part in range(2):
                y_sum = y_sum + dot(bd_ref[...], states[part * 8:part * 8 + 8].reshape(8 * CHANS, PATCH))
            return x_sum, y_sum

        x_sum, y_sum = lax.fori_loop(0, MEMBERS // GROUP, sums,
                                     (jnp.zeros((CHANS, PATCH), F32), jnp.zeros((8 * OBS, PATCH), F32)))
        xbar[...] = x_sum * (1.0 / MEMBERS)
        y_mean = jnp.sum(y_sum.reshape(OBS, 8, PATCH), axis=1) * (1.0 / MEMBERS)
        ybar[...] = y_mean
        root_wt = jnp.sqrt(wt_ref[row, my_half])
        sw_ref[...] = root_wt
        sd_ref[...] = root_wt * (yo_ref[row, my_half] - y_mean)

        def anomalies(group, carry):
            states = block(group)
            y_parts = [dot(bd_ref[...], states[part * 8:part * 8 + 8].reshape(8 * CHANS, PATCH)) for part in range(2)]
            spot = pl.ds(pl.multiple_of(group * GROUP, GROUP), GROUP)
            c_innov = jnp.zeros((GROUP, PATCH), F32)
            for o in range(OBS):
                y = jnp.concatenate([y_parts[0][o * 8:o * 8 + 8], y_parts[1][o * 8:o * 8 + 8]], axis=0)
                scaled = (y - ybar[o:o + 1]) * sw_ref[o:o + 1]
                c_innov = c_innov + scaled * sd_ref[o:o + 1]
                high, mid, low = split3(scaled)
                work[o, spot] = high
                work[OBS + o, spot] = mid
                work[2 * OBS + o, spot] = low
            cif[spot] = c_innov
            return carry

        lax.fori_loop(0, MEMBERS // GROUP, anomalies, 0)

        am[...] = jnp.zeros((MEMBERS, MEMBERS), F32)
        pm[...] = jnp.zeros((MEMBERS, MEMBERS), F32)

        def gram(o, carry):
            high = work[o]
            mid = work[OBS + o]
            pm[...] += dot_t(high, mid) + dot_t(high, work[2 * OBS + o])
            am[...] += dot_t(mid, mid) + dot_t(high, high)
            return carry

        lax.fori_loop(0, OBS, gram, 0)
        eye = jnp.where(row_id == col_id, 1.0, 0.0).astype(F32)
        cross = pm[...]
        a_mat = (MEMBERS - 1) * eye + (am[...] + (cross + cross.T))
        scale = jnp.sqrt(jnp.sum(jnp.sum(a_mat * a_mat, axis=0, keepdims=True), axis=1, keepdims=True))

        def put(refs, value):
            for index, part in enumerate(split3(value)):
                refs[index] = part

        def parts(refs):
            return [refs.at[index] for index in range(3)]

        put(sy, a_mat / scale)
        put(sz, eye)

        def newton(step, carry):
            unit = jnp.where(row_id == col_id, 1.5, 0.0).astype(F32)
            put(st, unit - 0.5 * dot6(parts(sz), parts(sy)))
            put(sy, dot6(parts(sy), parts(st)))
            z_next = dot6(parts(st), parts(sz))
            zm[...] = z_next
            put(sz, z_next)
            return carry

        lax.fori_loop(0, NS_STEPS, newton, 0)
        s_mat = zm[...] / jnp.sqrt(scale)
        zm[...] = s_mat
        put(sz, s_mat)
        pa_mat = dot6(parts(sz), parts(sz))
        c_innov = jnp.sum(cif[...], axis=1, keepdims=True)
        w_mean = jnp.sum(pa_mat * c_innov, axis=0, keepdims=True)
        t_mat = math.sqrt(MEMBERS - 1) * zm[...] + w_mean
        put(st, t_mat)
        rest = 1.0 - jnp.sum(t_mat, axis=1, keepdims=True)

        def by_channel(group, carry):
            spot = pl.ds(pl.multiple_of(group * GROUP, GROUP), GROUP)
            for part in range(2):
                piece = buf[OWNERS * chunk + group // SUBS, pl.ds((group % SUBS) * GROUP, GROUP), part * 16:part * 16 + 16]
                moved = dot(perm_ref[...], piece.reshape(256, PATCH)).astype(BF16)
                work[part * 16:part * 16 + 16, spot] = moved.reshape(16, 16, PATCH)
            return carry

        lax.fori_loop(0, MEMBERS // GROUP, by_channel, 0)

        def transform(c, carry):
            states = work[c]
            moved = dot(st[2], states) + dot(st[1], states) + dot(st[0], states)
            work[c] = (moved + rest * xbar[pl.ds(c, 1)]).astype(BF16)
            return carry

        lax.fori_loop(0, CHANS, transform, 0)

        for target in range(OWNERS):
            def by_member(index, carry):
                spot = pl.ds(pl.multiple_of(target * MINE + index * GROUP, GROUP), GROUP)
                for part in range(2):
                    piece = work[part * 16:part * 16 + 16, spot]
                    moved = dot(perm_ref[...], piece.reshape(256, PATCH)).astype(BF16)
                    xbuf[2 * chunk + target // 2, pl.ds(index * GROUP, GROUP), part * 16:part * 16 + 16,
                         (target % 2) * PATCH:(target % 2 + 1) * PATCH] = moved.reshape(16, 16, PATCH)
                return carry

            lax.fori_loop(0, SUBS, by_member, 0)

            @pl.when(me != target)
            def _():
                r_copy(chunk, target).start()

            @pl.when(me == target)
            def _():
                own_copy(chunk, target).start()
        return carry

    lax.fori_loop(0, CHUNKS, analyse, 0)

    def finish(chunk, carry):
        for t in range(1, OWNERS):
            f_copy(chunk, t, 0, MINE).wait_send()
            source = (me + t) % OWNERS
            pltpu.make_async_remote_copy(
                r_stage(chunk, 0), r_place(chunk, source), r_send.at[chunk, 0], r_recv.at[chunk, source],
                device_id={'ens': source}, device_id_type=MESH).wait_recv()
        for target in range(OWNERS):
            @pl.when(me != target)
            def _():
                r_copy(chunk, target).wait_send()

            @pl.when(me == target)
            def _():
                own_copy(chunk, target).wait()
        edge_copy(chunk).wait_send()
        return carry

    lax.fori_loop(0, CHUNKS, finish, 0)

    @pl.when(lat > 0)
    def _():
        send_up.wait_send()

    @pl.when(lat < lat_count - 1)
    def _():
        send_down.wait_send()


def solution(mesh):
    lat_count = mesh.shape['lat']
    dom_count = mesh.shape['dom']
    spots = np.arange(256)
    perm = np.zeros((256, 256), np.float32)
    perm[spots, (spots % 16) * 16 + spots // 16] = 1.0

    def local_cycle(ens_block, w_in, w_out, obs_op, obs_val, obs_wt):
        state = jnp.transpose(ens_block, (0, 1, 3, 2))
        op_t = jnp.transpose(obs_op)
        eye8 = jnp.eye(8, dtype=BF16)
        spread = (op_t[:, None, None, :] * eye8[None, :, :, None]).reshape(8 * OBS, 8 * CHANS)
        vmem = pl.BlockSpec(memory_space=pltpu.VMEM)
        hbm = pl.BlockSpec(memory_space=pl.ANY)
        result = pl.pallas_call(
            functools.partial(kernel, lat_count, dom_count),
            out_shape=jax.ShapeDtypeStruct(state.shape, BF16),
            in_specs=[vmem] * 6 + [hbm],
            out_specs=hbm,
            scratch_shapes=[
                pltpu.VMEM((STAGE + 3 * CHUNKS, MINE, CHANS, PATCH), BF16),
                pltpu.VMEM((ROWS + 2, MINE, CHANS, COLS), BF16),
                pltpu.VMEM((CHUNKS, 2, CHANS, 128), BF16),
                pltpu.VMEM((CHUNKS, 2, CHANS, 128), BF16),
                pltpu.VMEM((3 * OBS, MEMBERS, PATCH), BF16),
                pltpu.VMEM((MEMBERS, MEMBERS), F32),
                pltpu.VMEM((MEMBERS, MEMBERS), F32),
                pltpu.VMEM((MEMBERS, MEMBERS), F32),
                pltpu.VMEM((MEMBERS, MEMBERS), F32),
                pltpu.VMEM((3, MEMBERS, MEMBERS), BF16),
                pltpu.VMEM((3, MEMBERS, MEMBERS), BF16),
                pltpu.VMEM((3, MEMBERS, MEMBERS), BF16),
                pltpu.VMEM((CHANS, PATCH), F32),
                pltpu.VMEM((OBS, PATCH), F32),
                pltpu.VMEM((OBS, PATCH), F32),
                pltpu.VMEM((OBS, PATCH), F32),
                pltpu.SemaphoreType.DMA((ROWS,)),
                pltpu.SemaphoreType.DMA((2,)),
                pltpu.SemaphoreType.DMA((2,)),
                pltpu.SemaphoreType.DMA((2,)),
                pltpu.SemaphoreType.DMA((CHUNKS,)),
                pltpu.SemaphoreType.DMA((CHUNKS,)),
                pltpu.SemaphoreType.DMA((CHUNKS, 3)),
                pltpu.SemaphoreType.DMA((CHUNKS, OWNERS)),
                pltpu.SemaphoreType.DMA((CHUNKS, OWNERS)),
                pltpu.SemaphoreType.DMA((CHUNKS, OWNERS)),
                pltpu.SemaphoreType.DMA((CHUNKS,)),
            ],
            compiler_params=pltpu.CompilerParams(collective_id=0, has_side_effects=True, vmem_limit_bytes=67043328),
        )(jnp.transpose(w_in), jnp.transpose(w_out), spread, jnp.asarray(perm, BF16),
          jnp.transpose(obs_val, (0, 1, 3, 2)), jnp.transpose(obs_wt, (0, 1, 3, 2)), state)
        return jnp.transpose(result, (0, 1, 3, 2))

    state_spec = P('ens', 'lat', 'dom', None)
    obs_spec = P('lat', 'dom', None, None)
    return jax.shard_map(local_cycle, mesh=mesh, in_specs=(state_spec, P(), P(), P(), obs_spec, obs_spec), out_specs=state_spec, check_vma=False)
```

time: 1370 us -> 494 us (0.36)
  matrix products: 680 us -> 0 us
  Pallas kernels: 0 us -> 476 us
  local copies, waits for them, and re-layouts: 211 us -> 16.4 us
  blocking collectives: 187 us -> 0 us
  waiting for transfers between devices: 183 us -> 0 us
  other arithmetic: 80.6 us -> 0.78 us
  starting transfers between devices: 15.5 us -> 0 us
    dot_general x44 -> x0, matrix products: 680 us -> none  [the longest x1 323 us: value_a14(): jnp.einsum('mrwh,hc->mrwc', hidden, w_out, preferred_element_type=jnp.flo...]
    pallas_call x0 -> x1, Pallas kernels: none -> 476 us  [local_cycle(): pl.pallas_call(functools.partial(kernel, lat_count, dom_count), out_shape...]
    all_to_all x1 -> x0, blocking collectives: 187 us -> none  [local_cycle(): return lax.all_to_all(analysed, 'ens', 0, 1, tiled=True)]
    all_to_all x1 -> x0, waiting for transfers between devices: 183 us -> none  [local_cycle(): by_point = lax.all_to_all(value_a8, 'ens', 1, 0, tiled=True)]
    slice x4 -> x0, local copies, waits for them, and re-layouts: 61.6 us -> none  [the longest x1 27.6 us: value_a14(): block[:, :, 1:]]
    reshape x2 -> x0, local copies, waits for them, and re-layouts: 54.3 us -> none  [the longest x1 30.6 us: analyse_block(): x_anal.astype(jnp.bfloat16)]
    unnamed x1 -> x0, other arithmetic: 37.8 us -> none
    sub x3 -> x0, other arithmetic: 32 us -> none  [the longest x1 19.1 us: analyse_block(): x_anom = xf_patch.astype(jnp.float32) - x_mean]
  transfers between devices with their start and end apart: 5 -> 0, of which waited for: 1 -> 0; matrix products, arithmetic and copies ran while one was open for 10% -> 0% of each run, Pallas kernels for 0% -> 0%
where the time goes in v1:
time: 494 us; the launch traced here: 493 us
  Pallas kernels  476 us (96%)
  local copies, waits for them, and re-layouts  16.4 us (3%)
    pallas_call x1, Pallas kernels, local_cycle(): pl.pallas_call(functools.partial(kernel, lat_count, dom_count), out_shape...  476 us
    unnamed x2, local copies, waits for them, and re-layouts  15.6 us

profile of v1, /device:TPU:0, one launch (start us, length us, event | category | flops | bytes accessed | tf_op | source)
XLA Modules:
  0.0 493.3 jit_solution(1575888771266038524)
XLA Ops:
  0.0 1.4 copy.8
  1.4 0.8 broadcast_multiply_fusion
  2.2 0.8 mul.20.bd_ref
  3.0 476.1 %shard_map.73 = bf16[64,8,32,512]{3,2,1,0:T(8,128)(2,1)} custom-call(bf16[128,64]{1,0:T(8,128)(2,1)} %bitcast.13, bf16[32,128]{1,0:T(8,128)(2,1)} %bitcast.14, bf16[128,256]{1,0:T(8,128)(2,1)} %mul.20.bd_ref, bf16[256,256]{1,0:T(8,128)(2,1)} %constant.2.clone.perm_ref, f32[8,2,16,256]{3,2,1,0:T(8,128)} %bitcast.11, f32[8,2,16,256]{3,2,1,0:T(8,128)} %bitcast.12, ...), custom_call_target="tpu_custom_call" | custom-call | tf_op jit(solution)/shard_map/pallas_call | solution.py:397
  479.1 14.2 %copy.10 = bf16[64,8,512,32]{2,3,1,0:T(8,128)(2,1)} copy(bf16[64,8,512,32]{2,3,1,0:T(8,128)(2,1)} %bitcast.9) | data formatting | bytes 33554432
  (1 shorter events, 0.0 us)

commit v2 on v1

--- a/solution.py
+++ b/solution.py
@@ -23,6 +23,8 @@
 CHUNKS = 4
 OWNERS = 4
 GROUP = 16
+BATCH = 4
+PACK = 8
 SUBS = MINE // GROUP
 STAGE = CHUNKS * OWNERS
 
@@ -107,19 +109,21 @@
                                             device_id={'dom': dom_other}, device_id_type=MESH)
 
     def pack(chunk, carry):
-        def member(m, acc):
+        def members(index, acc):
             first, last = acc
-            for which in range(2):
-                row = chunk_row(chunk, which) + 1
-                spot = lane == which * MINE + m
-                west = xbuf[row, m, :, 0:128].astype(F32)
-                east = xbuf[row, m, :, COLS - 128:COLS].astype(F32)
-                first = jnp.where(spot, west[:, 0:1], first)
-                last = jnp.where(spot, east[:, 127:128], last)
+            for offset in range(PACK):
+                m = index * PACK + offset
+                for which in range(2):
+                    row = chunk_row(chunk, which) + 1
+                    spot = lane == which * MINE + m
+                    west = xbuf[row, m, :, 0:128].astype(F32)
+                    east = xbuf[row, m, :, COLS - 128:COLS].astype(F32)
+                    first = jnp.where(spot, west[:, 0:1], first)
+                    last = jnp.where(spot, east[:, 127:128], last)
             return first, last
 
         zero = jnp.zeros((CHANS, 128), F32)
-        first, last = lax.fori_loop(0, MINE, member, (zero, zero))
+        first, last = lax.fori_loop(0, MINE // PACK, members, (zero, zero))
         edge_out[chunk, 0] = first.astype(BF16)
         edge_out[chunk, 1] = last.astype(BF16)
         edge_copy(chunk).start()
@@ -163,35 +167,40 @@
             own = 1 - (ahead + OWNERS - 1) // OWNERS
             slots.append(own * (OWNERS * chunk + me) + (1 - own) * (STAGE + 3 * chunk + ahead - 1))
 
-        def member(m, carry):
+        def members(index, carry):
             from_east = edge_in[chunk, 0].astype(F32)
             from_west = edge_in[chunk, 1].astype(F32)
-            for which in range(2):
-                row = chunk_row(chunk, which) + 1
-                spot = which * MINE + m
-                halo_west = pltpu.roll(from_west, (128 - spot) % 128, 1)
-                halo_east = pltpu.roll(from_east, 127 - spot, 1)
-                here = xbuf[row, m]
-                mid = here.astype(F32)
-                above = xbuf[row - 1, m].astype(F32)
-                below = xbuf[row + 1, m].astype(F32)
-                west = pltpu.roll(mid, 1, 1)
-                east = pltpu.roll(mid, COLS - 1, 1)
-                west = jnp.concatenate([jnp.where(lane == 0, halo_west, west[:, :128]), west[:, 128:]], axis=1)
-                east = jnp.concatenate([east[:, :COLS - 128], jnp.where(lane == 127, halo_east, east[:, COLS - 128:])], axis=1)
-                laplace = (above + below + west + east - 4.0 * mid).astype(BF16)
+            places, kept, features = [], [], []
+            for m in [index * BATCH + offset for offset in range(BATCH)]:
+                for which in range(2):
+                    row = chunk_row(chunk, which) + 1
+                    spot = which * MINE + m
+                    halo_west = pltpu.roll(from_west, (128 - spot) % 128, 1)
+                    halo_east = pltpu.roll(from_east, 127 - spot, 1)
+                    here = xbuf[row, m]
+                    mid = here.astype(F32)
+                    above = xbuf[row - 1, m].astype(F32)
+                    below = xbuf[row + 1, m].astype(F32)
+                    west = pltpu.roll(mid, 1, 1)
+                    east = pltpu.roll(mid, COLS - 1, 1)
+                    west = jnp.concatenate([jnp.where(lane == 0, halo_west, west[:, :128]), west[:, 128:]], axis=1)
+                    east = jnp.concatenate([east[:, :COLS - 128], jnp.where(lane == 127, halo_east, east[:, COLS - 128:])], axis=1)
+                    laplace = (above + below + west + east - 4.0 * mid).astype(BF16)
+                    features.append(jnp.concatenate([here, laplace], axis=0))
+                    places.append((row, m, which))
+            pre_act = dot(w1_ref[...], jnp.concatenate(features, axis=1))
+            hidden = (0.5 * pre_act * (1.0 + lax.erf(pre_act * math.sqrt(0.5)))).astype(BF16)
+            update = dot(w2_ref[...], hidden)
+            for unit, (row, m, which) in enumerate(places):
                 for half in range(2):
-                    span = slice(half * PATCH, (half + 1) * PATCH)
-                    features = jnp.concatenate([here[:, span], laplace[:, span]], axis=0)
-                    pre_act = dot(w1_ref[...], features)
-                    hidden = (0.5 * pre_act * (1.0 + lax.erf(pre_act * math.sqrt(0.5)))).astype(BF16)
-                    update = dot(w2_ref[...], hidden)
-                    buf[slots[2 * which + half], m] = (mid[:, span] + update).astype(BF16)
+                    part = update[:, unit * COLS + half * PATCH:unit * COLS + (half + 1) * PATCH]
+                    mid = xbuf[row, m, :, half * PATCH:(half + 1) * PATCH].astype(F32)
+                    buf[slots[2 * which + half], m] = (mid + part).astype(BF16)
             return carry
 
         def sub(index, carry):
             start = index * GROUP
-            lax.fori_loop(start, start + GROUP, member, 0)
+            lax.fori_loop(index * (GROUP // BATCH), (index + 1) * (GROUP // BATCH), members, 0)
             for t in (2, 1, 3):
                 f_copy(chunk, t, start, GROUP).start()
             return carry

time: 494 us -> 396 us (0.80)
  Pallas kernels: 476 us -> 376 us
    pallas_call x1, Pallas kernels: 476 us -> 376 us  [local_cycle(): pl.pallas_call(functools.partial(kernel, lat_count, dom_count), out_shape...]
where the time goes in v2:
time: 396 us; the launch traced here: 393 us
  Pallas kernels  376 us (95%)
  local copies, waits for them, and re-layouts  16.4 us (4%)
    pallas_call x1, Pallas kernels, local_cycle(): pl.pallas_call(functools.partial(kernel, lat_count, dom_count), out_shape...  376 us
    unnamed x2, local copies, waits for them, and re-layouts  15.6 us

profile of v2, /device:TPU:0, one launch (start us, length us, event | category | flops | bytes accessed | tf_op | source)
XLA Modules:
  0.0 393.3 jit_solution(8433880373478996877)
XLA Ops:
  0.0 1.4 copy.8
  1.4 0.8 broadcast_multiply_fusion
  2.2 0.8 mul.20.bd_ref
  3.0 376.1 %shard_map.73 = bf16[64,8,32,512]{3,2,1,0:T(8,128)(2,1)} custom-call(bf16[128,64]{1,0:T(8,128)(2,1)} %bitcast.13, bf16[32,128]{1,0:T(8,128)(2,1)} %bitcast.14, bf16[128,256]{1,0:T(8,128)(2,1)} %mul.20.bd_ref, bf16[256,256]{1,0:T(8,128)(2,1)} %constant.2.clone.perm_ref, f32[8,2,16,256]{3,2,1,0:T(8,128)} %bitcast.11, f32[8,2,16,256]{3,2,1,0:T(8,128)} %bitcast.12, ...), custom_call_target="tpu_custom_call" | custom-call | tf_op jit(solution)/shard_map/pallas_call | solution.py:406
  379.2 14.2 %copy.10 = bf16[64,8,512,32]{2,3,1,0:T(8,128)(2,1)} copy(bf16[64,8,512,32]{2,3,1,0:T(8,128)(2,1)} %bitcast.9) | data formatting | bytes 33554432
  (1 shorter events, 0.0 us)

commit v3 on v2

--- a/solution.py
+++ b/solution.py
@@ -3,7 +3,6 @@
 
 import jax
 import jax.numpy as jnp
-import numpy as np
 from jax import lax
 from jax.experimental import pallas as pl
 from jax.experimental.pallas import tpu as pltpu
@@ -26,6 +25,7 @@
 BATCH = 4
 PACK = 8
 SUBS = MINE // GROUP
+FIRST_ROWS = (1, 2, 0, 3)
 STAGE = CHUNKS * OWNERS
 
 
@@ -55,9 +55,9 @@
     return (1 - last) * (1 + 2 * chunk + which) + last * (ROWS - 1) * which
 
 
-def kernel(lat_count, dom_count, w1_ref, w2_ref, bd_ref, perm_ref, yo_ref, wt_ref, x_ref, out_ref,
-           buf, xbuf, edge_out, edge_in, work, am, pm, zm, cif, sy, sz, st, xbar, ybar, sw_ref, sd_ref,
-           x_sem, halo_send, halo_recv, halo_local, edge_send, edge_recv, f_send, f_recv, r_send, r_recv, own_sem):
+def kernel(lat_count, dom_count, w_in_ref, w2_ref, op_ref, yo_hbm, wt_hbm, x_ref, xbuf,
+           buf, w1_ref, bd_ref, perm_ref, yo_ref, wt_ref, edge_out, edge_in, work, am, pm, zm, cif, sy, sz, st, xbar, ybar, sw_ref, sd_ref,
+           x_sem, halo_send, halo_recv, halo_local, edge_send, edge_recv, f_send, f_recv, r_send, r_recv, obs_sem, ready):
     me = lax.axis_index('ens')
     lat = lax.axis_index('lat')
     dom = lax.axis_index('dom')
@@ -68,7 +68,8 @@
     dom_other = (dom + 1) % dom_count
 
     row_copies = [pltpu.make_async_copy(x_ref.at[:, r], xbuf.at[r + 1], x_sem.at[r]) for r in range(ROWS)]
-    for r in range(ROWS):
+    obs_copies = [pltpu.make_async_copy(yo_hbm, yo_ref, obs_sem.at[0]), pltpu.make_async_copy(wt_hbm, wt_ref, obs_sem.at[1])]
+    for r in FIRST_ROWS:
         row_copies[r].start()
 
     barrier = pltpu.get_barrier_semaphore()
@@ -77,6 +78,18 @@
     pl.semaphore_signal(barrier, inc=1, device_id={'lat': lat_up}, device_id_type=MESH)
     pl.semaphore_signal(barrier, inc=1, device_id={'lat': lat_down}, device_id_type=MESH)
     pl.semaphore_signal(barrier, inc=1, device_id={'dom': dom_other}, device_id_type=MESH)
+
+    w1_ref[...] = w_in_ref[...].astype(F32).T.astype(BF16)
+    chan_id = lax.broadcasted_iota(jnp.int32, (CHANS, 8 * CHANS), 0)
+    slot_id = lax.broadcasted_iota(jnp.int32, (CHANS, 8 * CHANS), 1)
+    repeat = jnp.where(chan_id == slot_id % CHANS, 1.0, 0.0).astype(BF16)
+    wide = jnp.broadcast_to(dot(op_ref[...], repeat)[:, None, :], (OBS, 8, 8 * CHANS))
+    copy_id = lax.broadcasted_iota(jnp.int32, (OBS, 8, 8 * CHANS), 1)
+    place_id = lax.broadcasted_iota(jnp.int32, (OBS, 8, 8 * CHANS), 2)
+    bd_ref[...] = jnp.where(copy_id == place_id // CHANS, wide, 0.0).reshape(8 * OBS, 8 * CHANS).astype(BF16)
+    row_id = lax.broadcasted_iota(jnp.int32, (MEMBERS, MEMBERS), 0)
+    col_id = lax.broadcasted_iota(jnp.int32, (MEMBERS, MEMBERS), 1)
+    perm_ref[...] = jnp.where((row_id // 16 == col_id % 16) & (row_id % 16 == col_id // 16), 1.0, 0.0).astype(BF16)
     pl.semaphore_wait(barrier, OWNERS + 2)
 
     send_up = pltpu.make_async_remote_copy(x_ref.at[:, 0], xbuf.at[ROWS + 1], halo_send.at[0], halo_recv.at[1],
@@ -108,7 +121,7 @@
         return pltpu.make_async_remote_copy(edge_out.at[chunk], edge_in.at[chunk], edge_send.at[chunk], edge_recv.at[chunk],
                                             device_id={'dom': dom_other}, device_id_type=MESH)
 
-    def pack(chunk, carry):
+    def pack(chunk):
         def members(index, acc):
             first, last = acc
             for offset in range(PACK):
@@ -127,14 +140,18 @@
         edge_out[chunk, 0] = first.astype(BF16)
         edge_out[chunk, 1] = last.astype(BF16)
         edge_copy(chunk).start()
-        return carry
-
-    for r in range(4):
+
+    for r in (1, 2):
         row_copies[r].wait()
-    pack(0, 0)
+    pack(0)
+    for r in (0, 3):
+        row_copies[r].wait()
     for r in range(4, ROWS):
-        row_copies[r].wait()
-    lax.fori_loop(1, CHUNKS, pack, 0)
+        row_copies[r].start()
+    for copy in obs_copies:
+        copy.start()
+    row_copies[4].wait()
+    pack(1)
 
     def f_copy(chunk, t, start, size):
         owner = (me + t) % OWNERS
@@ -167,7 +184,7 @@
             own = 1 - (ahead + OWNERS - 1) // OWNERS
             slots.append(own * (OWNERS * chunk + me) + (1 - own) * (STAGE + 3 * chunk + ahead - 1))
 
-        def members(index, carry):
+        def members(index):
             from_east = edge_in[chunk, 0].astype(F32)
             from_west = edge_in[chunk, 1].astype(F32)
             places, kept, features = [], [], []
@@ -196,36 +213,39 @@
                     part = update[:, unit * COLS + half * PATCH:unit * COLS + (half + 1) * PATCH]
                     mid = xbuf[row, m, :, half * PATCH:(half + 1) * PATCH].astype(F32)
                     buf[slots[2 * which + half], m] = (mid + part).astype(BF16)
-            return carry
-
-        def sub(index, carry):
-            start = index * GROUP
-            lax.fori_loop(index * (GROUP // BATCH), (index + 1) * (GROUP // BATCH), members, 0)
+
+        def send(index, carry):
+            members(index)
             for t in (2, 1, 3):
-                f_copy(chunk, t, start, GROUP).start()
-            return carry
-
-        lax.fori_loop(0, SUBS, sub, 0)
+                f_copy(chunk, t, index * BATCH, BATCH).start()
+            return carry
+
+        lax.fori_loop(0, MINE // BATCH, send, 0)
+
+        @pl.when(chunk == 0)
+        def _():
+            for r in range(5, ROWS):
+                row_copies[r].wait()
+
+        @pl.when(chunk < CHUNKS - 2)
+        def _():
+            pack(chunk + 2)
         return carry
 
     lax.fori_loop(0, CHUNKS, forecast_chunk, 0)
-
-    def r_place(chunk, owner):
-        return out_ref.at[:, chunk_row(chunk, owner // 2), :, pl.ds(pl.multiple_of((owner % 2) * PATCH, PATCH), PATCH)]
-
-    def r_stage(chunk, target):
-        return xbuf.at[2 * chunk + target // 2, :, :, (target % 2) * PATCH:(target % 2 + 1) * PATCH]
-
-    def r_copy(chunk, target):
+    for t in range(1, OWNERS):
+        pl.semaphore_signal(ready, inc=1, device_id={'ens': (me + t) % OWNERS}, device_id_type=MESH)
+    for copy in obs_copies:
+        copy.wait()
+
+    def place(chunk, owner):
+        return chunk_row(chunk, owner // 2) + 1, pl.ds(pl.multiple_of((owner % 2) * PATCH, PATCH), PATCH)
+
+    def r_copy(chunk, t, source):
+        row, span = place(chunk, source)
         return pltpu.make_async_remote_copy(
-            r_stage(chunk, target), r_place(chunk, me), r_send.at[chunk, target], r_recv.at[chunk, me],
-            device_id={'ens': target}, device_id_type=MESH)
-
-    def own_copy(chunk, target):
-        return pltpu.make_async_copy(r_stage(chunk, target), r_place(chunk, me), own_sem.at[chunk])
-
-    row_id = lax.broadcasted_iota(jnp.int32, (MEMBERS, MEMBERS), 0)
-    col_id = lax.broadcasted_iota(jnp.int32, (MEMBERS, MEMBERS), 1)
+            buf.at[STAGE + 3 * chunk + t - 1], xbuf.at[row, :, :, span], r_send.at[chunk, t - 1], r_recv.at[chunk, source],
+            device_id={'ens': (me + t) % OWNERS}, device_id_type=MESH)
 
     def analyse(chunk, carry):
         for t in range(1, OWNERS):
@@ -337,44 +357,37 @@
 
         lax.fori_loop(0, CHANS, transform, 0)
 
-        for target in range(OWNERS):
+        for t in range(1, OWNERS):
+            f_copy(chunk, t, 0, MINE).wait_send()
+
+        @pl.when(chunk == 0)
+        def _():
+            pl.semaphore_wait(ready, OWNERS - 1)
+
+        for t in (2, 1, 3, 0):
             def by_member(index, carry):
-                spot = pl.ds(pl.multiple_of(target * MINE + index * GROUP, GROUP), GROUP)
+                spot = pl.ds(pl.multiple_of(((me + t) % OWNERS) * MINE + index * GROUP, GROUP), GROUP)
                 for part in range(2):
                     piece = work[part * 16:part * 16 + 16, spot]
-                    moved = dot(perm_ref[...], piece.reshape(256, PATCH)).astype(BF16)
-                    xbuf[2 * chunk + target // 2, pl.ds(index * GROUP, GROUP), part * 16:part * 16 + 16,
-                         (target % 2) * PATCH:(target % 2 + 1) * PATCH] = moved.reshape(16, 16, PATCH)
+                    moved = dot(perm_ref[...], piece.reshape(256, PATCH)).astype(BF16).reshape(16, 16, PATCH)
+                    if t == 0:
+                        own_row, own_span = place(chunk, me)
+                        xbuf[own_row, pl.ds(index * GROUP, GROUP), part * 16:part * 16 + 16, own_span] = moved
+                    else:
+                        buf[STAGE + 3 * chunk + t - 1, pl.ds(index * GROUP, GROUP), part * 16:part * 16 + 16] = moved
                 return carry
 
             lax.fori_loop(0, SUBS, by_member, 0)
-
-            @pl.when(me != target)
-            def _():
-                r_copy(chunk, target).start()
-
-            @pl.when(me == target)
-            def _():
-                own_copy(chunk, target).start()
+            if t:
+                r_copy(chunk, t, me).start()
         return carry
 
     lax.fori_loop(0, CHUNKS, analyse, 0)
 
     def finish(chunk, carry):
         for t in range(1, OWNERS):
-            f_copy(chunk, t, 0, MINE).wait_send()
-            source = (me + t) % OWNERS
-            pltpu.make_async_remote_copy(
-                r_stage(chunk, 0), r_place(chunk, source), r_send.at[chunk, 0], r_recv.at[chunk, source],
-                device_id={'ens': source}, device_id_type=MESH).wait_recv()
-        for target in range(OWNERS):
-            @pl.when(me != target)
-            def _():
-                r_copy(chunk, target).wait_send()
-
-            @pl.when(me == target)
-            def _():
-                own_copy(chunk, target).wait()
+            r_copy(chunk, t, (me + t) % OWNERS).wait_recv()
+            r_copy(chunk, t, me).wait_send()
         edge_copy(chunk).wait_send()
         return carry
 
@@ -387,30 +400,36 @@
     @pl.when(lat < lat_count - 1)
     def _():
         send_down.wait_send()
+
+
+def store_kernel(held, out_ref, sems):
+    copies = [pltpu.make_async_copy(held.at[r + 1], out_ref.at[:, r], sems.at[r]) for r in range(ROWS)]
+    for copy in copies:
+        copy.start()
+    for copy in copies:
+        copy.wait()
 
 
 def solution(mesh):
     lat_count = mesh.shape['lat']
     dom_count = mesh.shape['dom']
-    spots = np.arange(256)
-    perm = np.zeros((256, 256), np.float32)
-    perm[spots, (spots % 16) * 16 + spots // 16] = 1.0
 
     def local_cycle(ens_block, w_in, w_out, obs_op, obs_val, obs_wt):
         state = jnp.transpose(ens_block, (0, 1, 3, 2))
-        op_t = jnp.transpose(obs_op)
-        eye8 = jnp.eye(8, dtype=BF16)
-        spread = (op_t[:, None, None, :] * eye8[None, :, :, None]).reshape(8 * OBS, 8 * CHANS)
         vmem = pl.BlockSpec(memory_space=pltpu.VMEM)
         hbm = pl.BlockSpec(memory_space=pl.ANY)
-        result = pl.pallas_call(
+        held = pl.pallas_call(
             functools.partial(kernel, lat_count, dom_count),
-            out_shape=jax.ShapeDtypeStruct(state.shape, BF16),
-            in_specs=[vmem] * 6 + [hbm],
-            out_specs=hbm,
+            out_shape=pltpu.VMEM((ROWS + 2, MINE, CHANS, COLS), BF16),
+            in_specs=[vmem] * 3 + [hbm] * 3,
+            out_specs=vmem,
             scratch_shapes=[
                 pltpu.VMEM((STAGE + 3 * CHUNKS, MINE, CHANS, PATCH), BF16),
-                pltpu.VMEM((ROWS + 2, MINE, CHANS, COLS), BF16),
+                pltpu.VMEM((128, 2 * CHANS), BF16),
+                pltpu.VMEM((8 * OBS, 8 * CHANS), BF16),
+                pltpu.VMEM((256, 256), BF16),
+                pltpu.VMEM((ROWS, 2, OBS, PATCH), F32),
+                pltpu.VMEM((ROWS, 2, OBS, PATCH), F32),
                 pltpu.VMEM((CHUNKS, 2, CHANS, 128), BF16),
                 pltpu.VMEM((CHUNKS, 2, CHANS, 128), BF16),
                 pltpu.VMEM((3 * OBS, MEMBERS, PATCH), BF16),
@@ -433,13 +452,22 @@
                 pltpu.SemaphoreType.DMA((CHUNKS,)),
                 pltpu.SemaphoreType.DMA((CHUNKS, 3)),
                 pltpu.SemaphoreType.DMA((CHUNKS, OWNERS)),
+                pltpu.SemaphoreType.DMA((CHUNKS, 3)),
                 pltpu.SemaphoreType.DMA((CHUNKS, OWNERS)),
-                pltpu.SemaphoreType.DMA((CHUNKS, OWNERS)),
-                pltpu.SemaphoreType.DMA((CHUNKS,)),
+                pltpu.SemaphoreType.DMA((2,)),
+                pltpu.SemaphoreType.REGULAR,
             ],
-            compiler_params=pltpu.CompilerParams(collective_id=0, has_side_effects=True, vmem_limit_bytes=67043328),
-        )(jnp.transpose(w_in), jnp.transpose(w_out), spread, jnp.asarray(perm, BF16),
+            compiler_params=pltpu.CompilerParams(collective_id=0, has_side_effects=True, vmem_limit_bytes=43 * 2 ** 20),
+        )(w_in, jnp.transpose(w_out), jnp.transpose(obs_op),
           jnp.transpose(obs_val, (0, 1, 3, 2)), jnp.transpose(obs_wt, (0, 1, 3, 2)), state)
+        result = pl.pallas_call(
+            store_kernel,
+            out_shape=jax.ShapeDtypeStruct(state.shape, BF16),
+            in_specs=[vmem],
+            out_specs=hbm,
+            scratch_shapes=[pltpu.SemaphoreType.DMA((ROWS,))],
+            compiler_params=pltpu.CompilerParams(vmem_limit_bytes=2 ** 20),
+        )(pltpu.with_memory_space_constraint(held, pltpu.VMEM))
         return jnp.transpose(result, (0, 1, 3, 2))
 
     state_spec = P('ens', 'lat', 'dom', None)

time: 396 us -> 379 us (0.957)
  local copies, waits for them, and re-layouts: 16.4 us -> 0 us
    unnamed x2 -> x0, local copies, waits for them, and re-layouts: 15.6 us -> none
    pallas_call x0 -> x1, Pallas kernels: none -> 5.93 us  [local_cycle(): pl.pallas_call(store_kernel, out_shape=jax.ShapeDtypeStruct(state.shape,...]
    pallas_call x1, Pallas kernels: 376 us -> 372 us  [local_cycle(): pl.pallas_call(functools.partial(kernel, lat_count, dom_count), out_shape...]
where the time goes in v3:
time: 379 us; the launch traced here: 378 us
  Pallas kernels  378 us (100%)
    pallas_call x1, Pallas kernels, local_cycle(): pl.pallas_call(functools.partial(kernel, lat_count, dom_count), out_shape...  372 us

profile of v3, /device:TPU:0, one launch (start us, length us, event | category | flops | bytes accessed | tf_op | source)
XLA Modules:
  0.0 377.9 jit_solution(13498335626277712630)
XLA Ops:
  0.0 372.0 %shard_map.64.held = bf16[10,64,32,512]{3,2,1,0:T(8,128)(2,1)S(1)} custom-call(bf16[64,128]{1,0:T(8,128)(2,1)} %w_in_ref.1, bf16[32,128]{1,0:T(8,128)(2,1)} %bitcast.9, bf16[16,32]{1,0:T(8,128)(2,1)} %bitcast.10, f32[8,2,16,256]{3,2,1,0:T(8,128)} %bitcast.7, f32[8,2,16,256]{3,2,1,0:T(8,128)} %bitcast.8, bf16[64,8,32,512]{3,2,1,0:T(8,128)(2,1)} %bitcast.6), custom_call_target="tpu_custom_call" | custom-call | tf_op jit(solution)/shard_map/pallas_call | solution.py:421
  372.0 5.9 %shard_map.65 = bf16[64,8,32,512]{3,2,1,0:T(8,128)(2,1)} custom-call(bf16[10,64,32,512]{3,2,1,0:T(8,128)(2,1)S(1)} %shard_map.64.held), custom_call_target="tpu_custom_call" | custom-call | tf_op jit(solution)/shard_map/pallas_call | solution.py:463

commit v4 on v3

--- a/solution.py
+++ b/solution.py
@@ -25,7 +25,8 @@
 BATCH = 4
 PACK = 8
 SUBS = MINE // GROUP
-FIRST_ROWS = (1, 2, 0, 3)
+FIRST = 16
+INNER = 32
 STAGE = CHUNKS * OWNERS
 
 
@@ -55,9 +56,9 @@
     return (1 - last) * (1 + 2 * chunk + which) + last * (ROWS - 1) * which
 
 
-def kernel(lat_count, dom_count, w_in_ref, w2_ref, op_ref, yo_hbm, wt_hbm, x_ref, xbuf,
-           buf, w1_ref, bd_ref, perm_ref, yo_ref, wt_ref, edge_out, edge_in, work, am, pm, zm, cif, sy, sz, st, xbar, ybar, sw_ref, sd_ref,
-           x_sem, halo_send, halo_recv, halo_local, edge_send, edge_recv, f_send, f_recv, r_send, r_recv, obs_sem, ready):
+def kernel(lat_count, dom_count, w_in_hbm, w_out_hbm, op_hbm, yo_hbm, wt_hbm, x_ref, xbuf,
+           buf, w_in_ref, w2_ref, op_ref, w1_ref, bd_ref, perm_ref, yo_ref, wt_ref, edge_out, edge_in, work, am, pm, zm, cif, sy, sz, st, xbar, ybar, sw_ref, sd_ref,
+           first_sem, x_sem, small_sem, halo_send, halo_recv, halo_local, edge_send, edge_recv, f_send, f_recv, r_send, r_recv, obs_sem, ready):
     me = lax.axis_index('ens')
     lat = lax.axis_index('lat')
     dom = lax.axis_index('dom')
@@ -67,10 +68,14 @@
     lat_down = (lat + 1) % lat_count
     dom_other = (dom + 1) % dom_count
 
-    row_copies = [pltpu.make_async_copy(x_ref.at[:, r], xbuf.at[r + 1], x_sem.at[r]) for r in range(ROWS)]
+    first_copies = [pltpu.make_async_copy(x_ref.at[0:FIRST, r], xbuf.at[r + 1, 0:FIRST], first_sem.at[r]) for r in range(4)]
+    row_copies = [pltpu.make_async_copy(x_ref.at[FIRST:, r], xbuf.at[r + 1, FIRST:], x_sem.at[r]) for r in range(4)]
+    row_copies += [pltpu.make_async_copy(x_ref.at[:, r], xbuf.at[r + 1], x_sem.at[r]) for r in range(4, ROWS)]
+    small_copies = [pltpu.make_async_copy(source, target, small_sem.at[index]) for index, (source, target) in enumerate(
+        ((w_in_hbm, w_in_ref), (w_out_hbm, w2_ref), (op_hbm, op_ref)))]
     obs_copies = [pltpu.make_async_copy(yo_hbm, yo_ref, obs_sem.at[0]), pltpu.make_async_copy(wt_hbm, wt_ref, obs_sem.at[1])]
-    for r in FIRST_ROWS:
-        row_copies[r].start()
+    for copy in small_copies + first_copies:
+        copy.start()
 
     barrier = pltpu.get_barrier_semaphore()
     for t in range(1, OWNERS):
@@ -79,17 +84,9 @@
     pl.semaphore_signal(barrier, inc=1, device_id={'lat': lat_down}, device_id_type=MESH)
     pl.semaphore_signal(barrier, inc=1, device_id={'dom': dom_other}, device_id_type=MESH)
 
+    for copy in small_copies:
+        copy.wait()
     w1_ref[...] = w_in_ref[...].astype(F32).T.astype(BF16)
-    chan_id = lax.broadcasted_iota(jnp.int32, (CHANS, 8 * CHANS), 0)
-    slot_id = lax.broadcasted_iota(jnp.int32, (CHANS, 8 * CHANS), 1)
-    repeat = jnp.where(chan_id == slot_id % CHANS, 1.0, 0.0).astype(BF16)
-    wide = jnp.broadcast_to(dot(op_ref[...], repeat)[:, None, :], (OBS, 8, 8 * CHANS))
-    copy_id = lax.broadcasted_iota(jnp.int32, (OBS, 8, 8 * CHANS), 1)
-    place_id = lax.broadcasted_iota(jnp.int32, (OBS, 8, 8 * CHANS), 2)
-    bd_ref[...] = jnp.where(copy_id == place_id // CHANS, wide, 0.0).reshape(8 * OBS, 8 * CHANS).astype(BF16)
-    row_id = lax.broadcasted_iota(jnp.int32, (MEMBERS, MEMBERS), 0)
-    col_id = lax.broadcasted_iota(jnp.int32, (MEMBERS, MEMBERS), 1)
-    perm_ref[...] = jnp.where((row_id // 16 == col_id % 16) & (row_id % 16 == col_id // 16), 1.0, 0.0).astype(BF16)
     pl.semaphore_wait(barrier, OWNERS + 2)
 
     send_up = pltpu.make_async_remote_copy(x_ref.at[:, 0], xbuf.at[ROWS + 1], halo_send.at[0], halo_recv.at[1],
@@ -98,22 +95,6 @@
                                              device_id={'lat': lat_down}, device_id_type=MESH)
     top_copy = pltpu.make_async_copy(x_ref.at[:, 0], xbuf.at[0], halo_local.at[0])
     bottom_copy = pltpu.make_async_copy(x_ref.at[:, ROWS - 1], xbuf.at[ROWS + 1], halo_local.at[1])
-
-    @pl.when(lat > 0)
-    def _():
-        send_up.start()
-
-    @pl.when(lat < lat_count - 1)
-    def _():
-        send_down.start()
-
-    @pl.when(lat == 0)
-    def _():
-        top_copy.start()
-
-    @pl.when(lat == lat_count - 1)
-    def _():
-        bottom_copy.start()
 
     lane = lax.broadcasted_iota(jnp.int32, (CHANS, 128), 1)
 
@@ -141,23 +122,110 @@
         edge_out[chunk, 1] = last.astype(BF16)
         edge_copy(chunk).start()
 
-    for r in (1, 2):
-        row_copies[r].wait()
-    pack(0)
-    for r in (0, 3):
+    for copy in first_copies:
+        copy.wait()
+    for r in range(4):
+        row_copies[r].start()
+
+    def f_copy(chunk, t, start, size, kind='all'):
+        owner = (me + t) % OWNERS
+        source = buf.at[STAGE + 3 * chunk + t - 1, pl.ds(start, size)]
+        target = buf.at[OWNERS * chunk + me, pl.ds(start, size)]
+        if kind != 'all':
+            half = owner % 2 if kind == 'outer' else 1 - owner % 2
+            span = pl.ds(pl.multiple_of(half * 128, 128), 128)
+            source = source.at[:, :, span]
+            target = target.at[:, :, span]
+        return pltpu.make_async_remote_copy(source, target, f_send.at[chunk, t - 1], f_recv.at[chunk, me],
+                                            device_id={'ens': owner}, device_id_type=MESH)
+
+    def slots_of(chunk):
+        slots = []
+        for owner in range(OWNERS):
+            ahead = (owner - me + OWNERS) % OWNERS
+            own = 1 - (ahead + OWNERS - 1) // OWNERS
+            slots.append(own * (OWNERS * chunk + me) + (1 - own) * (STAGE + 3 * chunk + ahead - 1))
+        return slots
+
+    pieces_of = {'all': (PATCH, ((0, 0, 0), (PATCH, 0, 1))),
+                 'inner': (128, ((128, 128, 0), (PATCH, 0, 1))),
+                 'outer': (128, ((0, 0, 0), (PATCH + 128, 128, 1)))}
+
+    def members(chunk, index, kind):
+        width, pieces = pieces_of[kind]
+        slots = slots_of(chunk)
+        if kind != 'inner':
+            from_east = edge_in[chunk, 0].astype(F32)
+            from_west = edge_in[chunk, 1].astype(F32)
+        places, features = [], []
+        for m in [index * BATCH + offset for offset in range(BATCH)]:
+            for which in range(2):
+                row = chunk_row(chunk, which) + 1
+                spot = which * MINE + m
+                here = xbuf[row, m]
+                mid = here.astype(F32)
+                above = xbuf[row - 1, m].astype(F32)
+                below = xbuf[row + 1, m].astype(F32)
+                west = pltpu.roll(mid, 1, 1)
+                east = pltpu.roll(mid, COLS - 1, 1)
+                if kind != 'inner':
+                    halo_west = pltpu.roll(from_west, (128 - spot) % 128, 1)
+                    halo_east = pltpu.roll(from_east, 127 - spot, 1)
+                    west = jnp.concatenate([jnp.where(lane == 0, halo_west, west[:, :128]), west[:, 128:]], axis=1)
+                    east = jnp.concatenate([east[:, :COLS - 128], jnp.where(lane == 127, halo_east, east[:, COLS - 128:])], axis=1)
+                laplace = (above + below + west + east - 4.0 * mid).astype(BF16)
+                for column, first_lane, half in pieces:
+                    span = slice(column, column + width)
+                    features.append(jnp.concatenate([here[:, span], laplace[:, span]], axis=0))
+                    places.append((row, m, span, slice(first_lane, first_lane + width), slots[2 * which + half]))
+        pre_act = dot(w1_ref[...], jnp.concatenate(features, axis=1))
+        hidden = (0.5 * pre_act * (1.0 + lax.erf(pre_act * math.sqrt(0.5)))).astype(BF16)
+        update = dot(w2_ref[...], hidden)
+        for unit, (row, m, span, lanes, slot) in enumerate(places):
+            part = update[:, unit * width:(unit + 1) * width]
+            buf[slot, m, :, lanes] = (xbuf[row, m, :, span].astype(F32) + part).astype(BF16)
+
+    def forecast(chunk, start, stop, kind):
+        def step(index, carry):
+            members(chunk, index, kind)
+            for t in (2, 1, 3):
+                f_copy(chunk, t, index * BATCH, BATCH, kind).start()
+            return carry
+
+        lax.fori_loop(start // BATCH, stop // BATCH, step, 0)
+
+    forecast(0, 0, FIRST, 'inner')
+    for r in range(4):
         row_copies[r].wait()
     for r in range(4, ROWS):
         row_copies[r].start()
     for copy in obs_copies:
         copy.start()
-    row_copies[4].wait()
+    pack(0)
+
+    @pl.when(lat > 0)
+    def _():
+        send_up.start()
+
+    @pl.when(lat < lat_count - 1)
+    def _():
+        send_down.start()
+
+    @pl.when(lat == 0)
+    def _():
+        top_copy.start()
+
+    @pl.when(lat == lat_count - 1)
+    def _():
+        bottom_copy.start()
+
+    forecast(0, FIRST, INNER, 'inner')
+    edge_copy(0).wait_recv()
+    forecast(0, 0, INNER, 'outer')
+    forecast(0, INNER, MINE, 'all')
+    for r in range(4, ROWS):
+        row_copies[r].wait()
     pack(1)
-
-    def f_copy(chunk, t, start, size):
-        owner = (me + t) % OWNERS
-        return pltpu.make_async_remote_copy(
-            buf.at[STAGE + 3 * chunk + t - 1, pl.ds(start, size)], buf.at[OWNERS * chunk + me, pl.ds(start, size)],
-            f_send.at[chunk, t - 1], f_recv.at[chunk, me], device_id={'ens': owner}, device_id_type=MESH)
 
     def forecast_chunk(chunk, carry):
         edge_copy(chunk).wait_recv()
@@ -178,61 +246,25 @@
         def _():
             bottom_copy.wait()
 
-        slots = []
-        for owner in range(OWNERS):
-            ahead = (owner - me + OWNERS) % OWNERS
-            own = 1 - (ahead + OWNERS - 1) // OWNERS
-            slots.append(own * (OWNERS * chunk + me) + (1 - own) * (STAGE + 3 * chunk + ahead - 1))
-
-        def members(index):
-            from_east = edge_in[chunk, 0].astype(F32)
-            from_west = edge_in[chunk, 1].astype(F32)
-            places, kept, features = [], [], []
-            for m in [index * BATCH + offset for offset in range(BATCH)]:
-                for which in range(2):
-                    row = chunk_row(chunk, which) + 1
-                    spot = which * MINE + m
-                    halo_west = pltpu.roll(from_west, (128 - spot) % 128, 1)
-                    halo_east = pltpu.roll(from_east, 127 - spot, 1)
-                    here = xbuf[row, m]
-                    mid = here.astype(F32)
-                    above = xbuf[row - 1, m].astype(F32)
-                    below = xbuf[row + 1, m].astype(F32)
-                    west = pltpu.roll(mid, 1, 1)
-                    east = pltpu.roll(mid, COLS - 1, 1)
-                    west = jnp.concatenate([jnp.where(lane == 0, halo_west, west[:, :128]), west[:, 128:]], axis=1)
-                    east = jnp.concatenate([east[:, :COLS - 128], jnp.where(lane == 127, halo_east, east[:, COLS - 128:])], axis=1)
-                    laplace = (above + below + west + east - 4.0 * mid).astype(BF16)
-                    features.append(jnp.concatenate([here, laplace], axis=0))
-                    places.append((row, m, which))
-            pre_act = dot(w1_ref[...], jnp.concatenate(features, axis=1))
-            hidden = (0.5 * pre_act * (1.0 + lax.erf(pre_act * math.sqrt(0.5)))).astype(BF16)
-            update = dot(w2_ref[...], hidden)
-            for unit, (row, m, which) in enumerate(places):
-                for half in range(2):
-                    part = update[:, unit * COLS + half * PATCH:unit * COLS + (half + 1) * PATCH]
-                    mid = xbuf[row, m, :, half * PATCH:(half + 1) * PATCH].astype(F32)
-                    buf[slots[2 * which + half], m] = (mid + part).astype(BF16)
-
-        def send(index, carry):
-            members(index)
-            for t in (2, 1, 3):
-                f_copy(chunk, t, index * BATCH, BATCH).start()
-            return carry
-
-        lax.fori_loop(0, MINE // BATCH, send, 0)
-
-        @pl.when(chunk == 0)
+        @pl.when(chunk < CHUNKS - 1)
         def _():
-            for r in range(5, ROWS):
-                row_copies[r].wait()
-
-        @pl.when(chunk < CHUNKS - 2)
-        def _():
-            pack(chunk + 2)
+            pack(chunk + 1)
+
+        forecast(chunk, 0, MINE, 'all')
         return carry
 
-    lax.fori_loop(0, CHUNKS, forecast_chunk, 0)
+    lax.fori_loop(1, CHUNKS, forecast_chunk, 0)
+
+    chan_id = lax.broadcasted_iota(jnp.int32, (CHANS, 8 * CHANS), 0)
+    slot_id = lax.broadcasted_iota(jnp.int32, (CHANS, 8 * CHANS), 1)
+    repeat = jnp.where(chan_id == slot_id % CHANS, 1.0, 0.0).astype(BF16)
+    wide = jnp.broadcast_to(dot(op_ref[...], repeat)[:, None, :], (OBS, 8, 8 * CHANS))
+    copy_id = lax.broadcasted_iota(jnp.int32, (OBS, 8, 8 * CHANS), 1)
+    place_id = lax.broadcasted_iota(jnp.int32, (OBS, 8, 8 * CHANS), 2)
+    bd_ref[...] = jnp.where(copy_id == place_id // CHANS, wide, 0.0).reshape(8 * OBS, 8 * CHANS).astype(BF16)
+    row_id = lax.broadcasted_iota(jnp.int32, (MEMBERS, MEMBERS), 0)
+    col_id = lax.broadcasted_iota(jnp.int32, (MEMBERS, MEMBERS), 1)
+    perm_ref[...] = jnp.where((row_id // 16 == col_id % 16) & (row_id % 16 == col_id // 16), 1.0, 0.0).astype(BF16)
     for t in range(1, OWNERS):
         pl.semaphore_signal(ready, inc=1, device_id={'ens': (me + t) % OWNERS}, device_id_type=MESH)
     for copy in obs_copies:
@@ -421,10 +453,13 @@
         held = pl.pallas_call(
             functools.partial(kernel, lat_count, dom_count),
             out_shape=pltpu.VMEM((ROWS + 2, MINE, CHANS, COLS), BF16),
-            in_specs=[vmem] * 3 + [hbm] * 3,
+            in_specs=[hbm] * 6,
             out_specs=vmem,
             scratch_shapes=[
                 pltpu.VMEM((STAGE + 3 * CHUNKS, MINE, CHANS, PATCH), BF16),
+                pltpu.VMEM((2 * CHANS, 128), BF16),
+                pltpu.VMEM((CHANS, 128), BF16),
+                pltpu.VMEM((OBS, CHANS), BF16),
                 pltpu.VMEM((128, 2 * CHANS), BF16),
                 pltpu.VMEM((8 * OBS, 8 * CHANS), BF16),
                 pltpu.VMEM((256, 256), BF16),
@@ -444,7 +479,9 @@
                 pltpu.VMEM((OBS, PATCH), F32),
                 pltpu.VMEM((OBS, PATCH), F32),
                 pltpu.VMEM((OBS, PATCH), F32),
+                pltpu.SemaphoreType.DMA((4,)),
                 pltpu.SemaphoreType.DMA((ROWS,)),
+                pltpu.SemaphoreType.DMA((3,)),
                 pltpu.SemaphoreType.DMA((2,)),
                 pltpu.SemaphoreType.DMA((2,)),
                 pltpu.SemaphoreType.DMA((2,)),

time: 379 us -> 373 us (0.984)
  Pallas kernels: 378 us -> 373 us
    pallas_call x1, Pallas kernels: 372 us -> 367 us  [local_cycle(): pl.pallas_call(functools.partial(kernel, lat_count, dom_count), out_shape...]
where the time goes in v4:
time: 373 us
  Pallas kernels  373 us (100%)
    pallas_call x1, Pallas kernels, local_cycle(): pl.pallas_call(functools.partial(kernel, lat_count, dom_count), out_shape...  367 us

profile of v4, /device:TPU:0, one launch (start us, length us, event | category | flops | bytes accessed | tf_op | source)
XLA Modules:
  0.0 372.7 jit_solution(264864205243650638)
XLA Ops:
  0.0 366.8 %shard_map.64.held = bf16[10,64,32,512]{3,2,1,0:T(8,128)(2,1)S(1)} custom-call(bf16[64,128]{1,0:T(8,128)(2,1)} %w_in_hbm.1, bf16[32,128]{1,0:T(8,128)(2,1)} %bitcast.9, bf16[16,32]{1,0:T(8,128)(2,1)} %bitcast.10, f32[8,2,16,256]{3,2,1,0:T(8,128)} %bitcast.7, f32[8,2,16,256]{3,2,1,0:T(8,128)} %bitcast.8, bf16[64,8,32,512]{3,2,1,0:T(8,128)(2,1)} %bitcast.6), custom_call_target="tpu_custom_call" | custom-call | tf_op jit(solution)/shard_map/pallas_call | solution.py:453
  366.8 5.9 %shard_map.65 = bf16[64,8,32,512]{3,2,1,0:T(8,128)(2,1)} custom-call(bf16[10,64,32,512]{3,2,1,0:T(8,128)(2,1)S(1)} %shard_map.64.held), custom_call_target="tpu_custom_call" | custom-call | tf_op jit(solution)/shard_map/pallas_call | solution.py:500

commit v5 on v4

--- a/solution.py
+++ b/solution.py
@@ -58,7 +58,7 @@
 
 def kernel(lat_count, dom_count, w_in_hbm, w_out_hbm, op_hbm, yo_hbm, wt_hbm, x_ref, xbuf,
            buf, w_in_ref, w2_ref, op_ref, w1_ref, bd_ref, perm_ref, yo_ref, wt_ref, edge_out, edge_in, work, am, pm, zm, cif, sy, sz, st, xbar, ybar, sw_ref, sd_ref,
-           first_sem, x_sem, small_sem, halo_send, halo_recv, halo_local, edge_send, edge_recv, f_send, f_recv, r_send, r_recv, obs_sem, ready):
+           first_sem, upper_sem, lower_sem, small_sem, halo_send, halo_recv, halo_local, edge_send, edge_recv, f_send, f_recv, r_send, r_recv, obs_sem, ready):
     me = lax.axis_index('ens')
     lat = lax.axis_index('lat')
     dom = lax.axis_index('dom')
@@ -68,14 +68,26 @@
     lat_down = (lat + 1) % lat_count
     dom_other = (dom + 1) % dom_count
 
-    first_copies = [pltpu.make_async_copy(x_ref.at[0:FIRST, r], xbuf.at[r + 1, 0:FIRST], first_sem.at[r]) for r in range(4)]
-    row_copies = [pltpu.make_async_copy(x_ref.at[FIRST:, r], xbuf.at[r + 1, FIRST:], x_sem.at[r]) for r in range(4)]
-    row_copies += [pltpu.make_async_copy(x_ref.at[:, r], xbuf.at[r + 1], x_sem.at[r]) for r in range(4, ROWS)]
+    def first_copy(index):
+        some = pl.ds(index * BATCH, BATCH)
+        return pltpu.make_async_copy(x_ref.at[some, 0:4], xbuf.at[some, 1:5], first_sem.at[index])
+
+    def block_copies(start, first_row, sems):
+        size = (MINE - start) // 4
+        return [pltpu.make_async_copy(x_ref.at[start + size * part:start + size * part + size, first_row:first_row + 4],
+                                      xbuf.at[start + size * part:start + size * part + size, first_row + 1:first_row + 5],
+                                      sems.at[part]) for part in range(4)]
+
+    upper_copies = block_copies(FIRST, 0, upper_sem)
+    lower_copies = block_copies(0, 4, lower_sem)
     small_copies = [pltpu.make_async_copy(source, target, small_sem.at[index]) for index, (source, target) in enumerate(
         ((w_in_hbm, w_in_ref), (w_out_hbm, w2_ref), (op_hbm, op_ref)))]
     obs_copies = [pltpu.make_async_copy(yo_hbm, yo_ref, obs_sem.at[0]), pltpu.make_async_copy(wt_hbm, wt_ref, obs_sem.at[1])]
-    for copy in small_copies + first_copies:
+    first_copy(0).start()
+    for copy in small_copies:
         copy.start()
+    for index in range(1, FIRST // BATCH):
+        first_copy(index).start()
 
     barrier = pltpu.get_barrier_semaphore()
     for t in range(1, OWNERS):
@@ -89,12 +101,12 @@
     w1_ref[...] = w_in_ref[...].astype(F32).T.astype(BF16)
     pl.semaphore_wait(barrier, OWNERS + 2)
 
-    send_up = pltpu.make_async_remote_copy(x_ref.at[:, 0], xbuf.at[ROWS + 1], halo_send.at[0], halo_recv.at[1],
+    send_up = pltpu.make_async_remote_copy(x_ref.at[:, 0], xbuf.at[:, ROWS + 1], halo_send.at[0], halo_recv.at[1],
                                            device_id={'lat': lat_up}, device_id_type=MESH)
-    send_down = pltpu.make_async_remote_copy(x_ref.at[:, ROWS - 1], xbuf.at[0], halo_send.at[1], halo_recv.at[0],
+    send_down = pltpu.make_async_remote_copy(x_ref.at[:, ROWS - 1], xbuf.at[:, 0], halo_send.at[1], halo_recv.at[0],
                                              device_id={'lat': lat_down}, device_id_type=MESH)
-    top_copy = pltpu.make_async_copy(x_ref.at[:, 0], xbuf.at[0], halo_local.at[0])
-    bottom_copy = pltpu.make_async_copy(x_ref.at[:, ROWS - 1], xbuf.at[ROWS + 1], halo_local.at[1])
+    top_copy = pltpu.make_async_copy(x_ref.at[:, 0], xbuf.at[:, 0], halo_local.at[0])
+    bottom_copy = pltpu.make_async_copy(x_ref.at[:, ROWS - 1], xbuf.at[:, ROWS + 1], halo_local.at[1])
 
     lane = lax.broadcasted_iota(jnp.int32, (CHANS, 128), 1)
 
@@ -110,8 +122,8 @@
                 for which in range(2):
                     row = chunk_row(chunk, which) + 1
                     spot = lane == which * MINE + m
-                    west = xbuf[row, m, :, 0:128].astype(F32)
-                    east = xbuf[row, m, :, COLS - 128:COLS].astype(F32)
+                    west = xbuf[m, row, :, 0:128].astype(F32)
+                    east = xbuf[m, row, :, COLS - 128:COLS].astype(F32)
                     first = jnp.where(spot, west[:, 0:1], first)
                     last = jnp.where(spot, east[:, 127:128], last)
             return first, last
@@ -122,10 +134,8 @@
         edge_out[chunk, 1] = last.astype(BF16)
         edge_copy(chunk).start()
 
-    for copy in first_copies:
-        copy.wait()
-    for r in range(4):
-        row_copies[r].start()
+    for copy in upper_copies:
+        copy.start()
 
     def f_copy(chunk, t, start, size, kind='all'):
         owner = (me + t) % OWNERS
@@ -162,10 +172,10 @@
             for which in range(2):
                 row = chunk_row(chunk, which) + 1
                 spot = which * MINE + m
-                here = xbuf[row, m]
+                here = xbuf[m, row]
                 mid = here.astype(F32)
-                above = xbuf[row - 1, m].astype(F32)
-                below = xbuf[row + 1, m].astype(F32)
+                above = xbuf[m, row - 1].astype(F32)
+                below = xbuf[m, row + 1].astype(F32)
                 west = pltpu.roll(mid, 1, 1)
                 east = pltpu.roll(mid, COLS - 1, 1)
                 if kind != 'inner':
@@ -183,10 +193,12 @@
         update = dot(w2_ref[...], hidden)
         for unit, (row, m, span, lanes, slot) in enumerate(places):
             part = update[:, unit * width:(unit + 1) * width]
-            buf[slot, m, :, lanes] = (xbuf[row, m, :, span].astype(F32) + part).astype(BF16)
+            buf[slot, m, :, lanes] = (xbuf[m, row, :, span].astype(F32) + part).astype(BF16)
 
     def forecast(chunk, start, stop, kind):
         def step(index, carry):
+            if kind == 'inner' and start == 0:
+                first_copy(index).wait()
             members(chunk, index, kind)
             for t in (2, 1, 3):
                 f_copy(chunk, t, index * BATCH, BATCH, kind).start()
@@ -195,10 +207,10 @@
         lax.fori_loop(start // BATCH, stop // BATCH, step, 0)
 
     forecast(0, 0, FIRST, 'inner')
-    for r in range(4):
-        row_copies[r].wait()
-    for r in range(4, ROWS):
-        row_copies[r].start()
+    for copy in upper_copies:
+        copy.wait()
+    for copy in lower_copies:
+        copy.start()
     for copy in obs_copies:
         copy.start()
     pack(0)
@@ -223,8 +235,8 @@
     edge_copy(0).wait_recv()
     forecast(0, 0, INNER, 'outer')
     forecast(0, INNER, MINE, 'all')
-    for r in range(4, ROWS):
-        row_copies[r].wait()
+    for copy in lower_copies:
+        copy.wait()
     pack(1)
 
     def forecast_chunk(chunk, carry):
@@ -276,7 +288,7 @@
     def r_copy(chunk, t, source):
         row, span = place(chunk, source)
         return pltpu.make_async_remote_copy(
-            buf.at[STAGE + 3 * chunk + t - 1], xbuf.at[row, :, :, span], r_send.at[chunk, t - 1], r_recv.at[chunk, source],
+            buf.at[STAGE + 3 * chunk + t - 1], xbuf.at[:, row, :, span], r_send.at[chunk, t - 1], r_recv.at[chunk, source],
             device_id={'ens': (me + t) % OWNERS}, device_id_type=MESH)
 
     def analyse(chunk, carry):
@@ -404,7 +416,7 @@
                     moved = dot(perm_ref[...], piece.reshape(256, PATCH)).astype(BF16).reshape(16, 16, PATCH)
                     if t == 0:
                         own_row, own_span = place(chunk, me)
-                        xbuf[own_row, pl.ds(index * GROUP, GROUP), part * 16:part * 16 + 16, own_span] = moved
+                        xbuf[pl.ds(index * GROUP, GROUP), own_row, part * 16:part * 16 + 16, own_span] = moved
                     else:
                         buf[STAGE + 3 * chunk + t - 1, pl.ds(index * GROUP, GROUP), part * 16:part * 16 + 16] = moved
                 return carry
@@ -435,7 +447,9 @@
 
 
 def store_kernel(held, out_ref, sems):
-    copies = [pltpu.make_async_copy(held.at[r + 1], out_ref.at[:, r], sems.at[r]) for r in range(ROWS)]
+    size = MINE // ROWS
+    copies = [pltpu.make_async_copy(held.at[part * size:part * size + size, 1:ROWS + 1], out_ref.at[part * size:part * size + size], sems.at[part])
+              for part in range(ROWS)]
     for copy in copies:
         copy.start()
     for copy in copies:
@@ -452,7 +466,7 @@
         hbm = pl.BlockSpec(memory_space=pl.ANY)
         held = pl.pallas_call(
             functools.partial(kernel, lat_count, dom_count),
-            out_shape=pltpu.VMEM((ROWS + 2, MINE, CHANS, COLS), BF16),
+            out_shape=pltpu.VMEM((MINE, ROWS + 2, CHANS, COLS), BF16),
             in_specs=[hbm] * 6,
             out_specs=vmem,
             scratch_shapes=[
@@ -479,8 +493,9 @@
                 pltpu.VMEM((OBS, PATCH), F32),
                 pltpu.VMEM((OBS, PATCH), F32),
                 pltpu.VMEM((OBS, PATCH), F32),
+                pltpu.SemaphoreType.DMA((FIRST // BATCH,)),
                 pltpu.SemaphoreType.DMA((4,)),
-                pltpu.SemaphoreType.DMA((ROWS,)),
+                pltpu.SemaphoreType.DMA((4,)),
                 pltpu.SemaphoreType.DMA((3,)),
                 pltpu.SemaphoreType.DMA((2,)),
                 pltpu.SemaphoreType.DMA((2,)),

time: 373 us -> 373 us (level)
  no operation moved by 1% of the time
where the time goes in v5:
time: 373 us
  Pallas kernels  373 us (100%)
    pallas_call x1, Pallas kernels, local_cycle(): pl.pallas_call(functools.partial(kernel, lat_count, dom_count), out_shape...  367 us

profile of v5, /device:TPU:0, one launch (start us, length us, event | category | flops | bytes accessed | tf_op | source)
XLA Modules:
  0.0 372.7 jit_solution(12035487323702195551)
XLA Ops:
  0.0 366.8 %shard_map.64.held = bf16[64,10,32,512]{3,2,1,0:T(8,128)(2,1)S(1)} custom-call(bf16[64,128]{1,0:T(8,128)(2,1)} %w_in_hbm.1, bf16[32,128]{1,0:T(8,128)(2,1)} %bitcast.9, bf16[16,32]{1,0:T(8,128)(2,1)} %bitcast.10, f32[8,2,16,256]{3,2,1,0:T(8,128)} %bitcast.7, f32[8,2,16,256]{3,2,1,0:T(8,128)} %bitcast.8, bf16[64,8,32,512]{3,2,1,0:T(8,128)(2,1)} %bitcast.6), custom_call_target="tpu_custom_call" | custom-call | tf_op jit(solution)/shard_map/pallas_call | solution.py:467
  366.8 5.9 %shard_map.65 = bf16[64,8,32,512]{3,2,1,0:T(8,128)(2,1)} custom-call(bf16[64,10,32,512]{3,2,1,0:T(8,128)(2,1)S(1)} %shard_map.64.held), custom_call_target="tpu_custom_call" | custom-call | tf_op jit(solution)/shard_map/pallas_call | solution.py:515

commit v6 on v5

--- a/solution.py
+++ b/solution.py
@@ -24,6 +24,7 @@
 GROUP = 16
 BATCH = 4
 PACK = 8
+STORES = 32
 SUBS = MINE // GROUP
 FIRST = 16
 INNER = 32
@@ -99,7 +100,6 @@
     for copy in small_copies:
         copy.wait()
     w1_ref[...] = w_in_ref[...].astype(F32).T.astype(BF16)
-    pl.semaphore_wait(barrier, OWNERS + 2)
 
     send_up = pltpu.make_async_remote_copy(x_ref.at[:, 0], xbuf.at[:, ROWS + 1], halo_send.at[0], halo_recv.at[1],
                                            device_id={'lat': lat_up}, device_id_type=MESH)
@@ -134,9 +134,6 @@
         edge_out[chunk, 1] = last.astype(BF16)
         edge_copy(chunk).start()
 
-    for copy in upper_copies:
-        copy.start()
-
     def f_copy(chunk, t, start, size, kind='all'):
         owner = (me + t) % OWNERS
         source = buf.at[STAGE + 3 * chunk + t - 1, pl.ds(start, size)]
@@ -161,14 +158,14 @@
                  'inner': (128, ((128, 128, 0), (PATCH, 0, 1))),
                  'outer': (128, ((0, 0, 0), (PATCH + 128, 128, 1)))}
 
-    def members(chunk, index, kind):
+    def members(chunk, start, size, kind):
         width, pieces = pieces_of[kind]
         slots = slots_of(chunk)
         if kind != 'inner':
             from_east = edge_in[chunk, 0].astype(F32)
             from_west = edge_in[chunk, 1].astype(F32)
         places, features = [], []
-        for m in [index * BATCH + offset for offset in range(BATCH)]:
+        for m in [start + offset for offset in range(size)]:
             for which in range(2):
                 row = chunk_row(chunk, which) + 1
                 spot = which * MINE + m
@@ -195,18 +192,29 @@
             part = update[:, unit * width:(unit + 1) * width]
             buf[slot, m, :, lanes] = (xbuf[m, row, :, span].astype(F32) + part).astype(BF16)
 
+    def send(chunk, start, size, kind):
+        for t in (2, 1, 3):
+            f_copy(chunk, t, start, size, kind).start()
+
     def forecast(chunk, start, stop, kind):
         def step(index, carry):
-            if kind == 'inner' and start == 0:
+            if kind == 'inner' and start == BATCH:
                 first_copy(index).wait()
-            members(chunk, index, kind)
-            for t in (2, 1, 3):
-                f_copy(chunk, t, index * BATCH, BATCH, kind).start()
+            members(chunk, index * BATCH, BATCH, kind)
+            send(chunk, index * BATCH, BATCH, kind)
             return carry
 
         lax.fori_loop(start // BATCH, stop // BATCH, step, 0)
 
-    forecast(0, 0, FIRST, 'inner')
+    first_copy(0).wait()
+    members(0, 0, BATCH // 2, 'inner')
+    pl.semaphore_wait(barrier, OWNERS + 2)
+    send(0, 0, BATCH // 2, 'inner')
+    for copy in upper_copies:
+        copy.start()
+    members(0, BATCH // 2, BATCH // 2, 'inner')
+    send(0, BATCH // 2, BATCH // 2, 'inner')
+    forecast(0, BATCH, FIRST, 'inner')
     for copy in upper_copies:
         copy.wait()
     for copy in lower_copies:
@@ -447,9 +455,9 @@
 
 
 def store_kernel(held, out_ref, sems):
-    size = MINE // ROWS
+    size = MINE // STORES
     copies = [pltpu.make_async_copy(held.at[part * size:part * size + size, 1:ROWS + 1], out_ref.at[part * size:part * size + size], sems.at[part])
-              for part in range(ROWS)]
+              for part in range(STORES)]
     for copy in copies:
         copy.start()
     for copy in copies:
@@ -517,7 +525,7 @@
             out_shape=jax.ShapeDtypeStruct(state.shape, BF16),
             in_specs=[vmem],
             out_specs=hbm,
-            scratch_shapes=[pltpu.SemaphoreType.DMA((ROWS,))],
+            scratch_shapes=[pltpu.SemaphoreType.DMA((STORES,))],
             compiler_params=pltpu.CompilerParams(vmem_limit_bytes=2 ** 20),
         )(pltpu.with_memory_space_constraint(held, pltpu.VMEM))
         return jnp.transpose(result, (0, 1, 3, 2))

time: 373 us -> 373 us (level)
  no operation moved by 1% of the time
where the time goes in v6:
time: 373 us
  Pallas kernels  373 us (100%)
    pallas_call x1, Pallas kernels, local_cycle(): pl.pallas_call(functools.partial(kernel, lat_count, dom_count), out_shape...  367 us

profile of v6, /device:TPU:0, one launch (start us, length us, event | category | flops | bytes accessed | tf_op | source)
XLA Modules:
  0.0 373.0 jit_solution(13871178309616523488)
XLA Ops:
  0.0 366.9 %shard_map.64.held = bf16[64,10,32,512]{3,2,1,0:T(8,128)(2,1)S(1)} custom-call(bf16[64,128]{1,0:T(8,128)(2,1)} %w_in_hbm.1, bf16[32,128]{1,0:T(8,128)(2,1)} %bitcast.9, bf16[16,32]{1,0:T(8,128)(2,1)} %bitcast.10, f32[8,2,16,256]{3,2,1,0:T(8,128)} %bitcast.7, f32[8,2,16,256]{3,2,1,0:T(8,128)} %bitcast.8, bf16[64,8,32,512]{3,2,1,0:T(8,128)(2,1)} %bitcast.6), custom_call_target="tpu_custom_call" | custom-call | tf_op jit(solution)/shard_map/pallas_call | solution.py:475
  366.9 6.1 %shard_map.65 = bf16[64,8,32,512]{3,2,1,0:T(8,128)(2,1)} custom-call(bf16[64,10,32,512]{3,2,1,0:T(8,128)(2,1)S(1)} %shard_map.64.held), custom_call_target="tpu_custom_call" | custom-call | tf_op jit(solution)/shard_map/pallas_call | solution.py:523

commit v7 on v6

--- a/solution.py
+++ b/solution.py
@@ -24,7 +24,9 @@
 GROUP = 16
 BATCH = 4
 PACK = 8
-STORES = 32
+STORES = 8
+TAIL = 8
+MAIN = MINE - TAIL
 SUBS = MINE // GROUP
 FIRST = 16
 INNER = 32
@@ -57,9 +59,9 @@
     return (1 - last) * (1 + 2 * chunk + which) + last * (ROWS - 1) * which
 
 
-def kernel(lat_count, dom_count, w_in_hbm, w_out_hbm, op_hbm, yo_hbm, wt_hbm, x_ref, xbuf,
+def kernel(lat_count, dom_count, w_in_hbm, w_out_hbm, op_hbm, yo_hbm, wt_hbm, x_ref, xbuf, tail_a, tail_b,
            buf, w_in_ref, w2_ref, op_ref, w1_ref, bd_ref, perm_ref, yo_ref, wt_ref, edge_out, edge_in, work, am, pm, zm, cif, sy, sz, st, xbar, ybar, sw_ref, sd_ref,
-           first_sem, upper_sem, lower_sem, small_sem, halo_send, halo_recv, halo_local, edge_send, edge_recv, f_send, f_recv, r_send, r_recv, obs_sem, ready):
+           first_sem, upper_sem, lower_sem, small_sem, halo_send, halo_recv, halo_local, edge_send, edge_recv, f_send, f_recv, r_send, r_recv, last_send, last_recv, tail_sem, obs_sem, ready):
     me = lax.axis_index('ens')
     lat = lax.axis_index('lat')
     dom = lax.axis_index('dom')
@@ -296,8 +298,24 @@
     def r_copy(chunk, t, source):
         row, span = place(chunk, source)
         return pltpu.make_async_remote_copy(
-            buf.at[STAGE + 3 * chunk + t - 1], xbuf.at[:, row, :, span], r_send.at[chunk, t - 1], r_recv.at[chunk, source],
+            buf.at[STAGE + 3 * chunk + t - 1, 0:MAIN], xbuf.at[0:MAIN, row, :, span],
+            r_send.at[chunk, t - 1], r_recv.at[chunk, source],
             device_id={'ens': (me + t) % OWNERS}, device_id_type=MESH)
+
+    def last_copy(chunk, t, source):
+        row, span = place(chunk, source)
+        return pltpu.make_async_remote_copy(
+            buf.at[STAGE + 3 * chunk + t - 1, MAIN:MINE], xbuf.at[MAIN:MINE, row, :, span],
+            last_send.at[chunk, t - 1], last_recv.at[chunk, source],
+            device_id={'ens': (me + t) % OWNERS}, device_id_type=MESH)
+
+    def tail_copy(chunk, t):
+        source = buf.at[STAGE + 3 * chunk + t - 1, MAIN:MINE]
+        return pltpu.make_async_copy(source, tail_a if t == 2 else tail_b, tail_sem.at[0 if t == 2 else 1])
+
+    def leaves(chunk, t):
+        crosses = {1: me % 2, 2: 1, 3: 1 - me % 2}[t]
+        return (chunk // (CHUNKS - 1)) * crosses == 1
 
     def analyse(chunk, carry):
         for t in range(1, OWNERS):
@@ -432,6 +450,14 @@
             lax.fori_loop(0, SUBS, by_member, 0)
             if t:
                 r_copy(chunk, t, me).start()
+
+                @pl.when(leaves(chunk, t))
+                def _():
+                    tail_copy(chunk, t).start()
+
+                @pl.when(jnp.logical_not(leaves(chunk, t)))
+                def _():
+                    last_copy(chunk, t, me).start()
         return carry
 
     lax.fori_loop(0, CHUNKS, analyse, 0)
@@ -440,6 +466,15 @@
         for t in range(1, OWNERS):
             r_copy(chunk, t, (me + t) % OWNERS).wait_recv()
             r_copy(chunk, t, me).wait_send()
+
+            @pl.when(leaves(chunk, t))
+            def _():
+                tail_copy(chunk, t).wait()
+
+            @pl.when(jnp.logical_not(leaves(chunk, t)))
+            def _():
+                last_copy(chunk, t, (me + t) % OWNERS).wait_recv()
+                last_copy(chunk, t, me).wait_send()
         edge_copy(chunk).wait_send()
         return carry
 
@@ -464,6 +499,19 @@
         copy.wait()
 
 
+def join_kernel(whole, piece_a, piece_b, out_ref, sems):
+    me = lax.axis_index('ens')
+    copies = []
+    for index, (piece, source) in enumerate(((piece_a, (me + 2) % OWNERS), (piece_b, OWNERS - 1 - me))):
+        span = pl.ds(pl.multiple_of((source % 2) * PATCH, PATCH), PATCH)
+        row = chunk_row(CHUNKS - 1, source // 2)
+        copies.append(pltpu.make_async_copy(piece, out_ref.at[MAIN:MINE, row, :, span], sems.at[index]))
+    for copy in copies:
+        copy.start()
+    for copy in copies:
+        copy.wait()
+
+
 def solution(mesh):
     lat_count = mesh.shape['lat']
     dom_count = mesh.shape['dom']
@@ -472,11 +520,12 @@
         state = jnp.transpose(ens_block, (0, 1, 3, 2))
         vmem = pl.BlockSpec(memory_space=pltpu.VMEM)
         hbm = pl.BlockSpec(memory_space=pl.ANY)
-        held = pl.pallas_call(
+        tail = jax.ShapeDtypeStruct((TAIL, CHANS, PATCH), BF16)
+        held, tail_a, tail_b = pl.pallas_call(
             functools.partial(kernel, lat_count, dom_count),
-            out_shape=pltpu.VMEM((MINE, ROWS + 2, CHANS, COLS), BF16),
+            out_shape=(pltpu.VMEM((MINE, ROWS + 2, CHANS, COLS), BF16), tail, tail),
             in_specs=[hbm] * 6,
-            out_specs=vmem,
+            out_specs=(vmem, hbm, hbm),
             scratch_shapes=[
                 pltpu.VMEM((STAGE + 3 * CHUNKS, MINE, CHANS, PATCH), BF16),
                 pltpu.VMEM((2 * CHANS, 128), BF16),
@@ -514,12 +563,17 @@
                 pltpu.SemaphoreType.DMA((CHUNKS, OWNERS)),
                 pltpu.SemaphoreType.DMA((CHUNKS, 3)),
                 pltpu.SemaphoreType.DMA((CHUNKS, OWNERS)),
+                pltpu.SemaphoreType.DMA((CHUNKS, 3)),
+                pltpu.SemaphoreType.DMA((CHUNKS, OWNERS)),
+                pltpu.SemaphoreType.DMA((2,)),
                 pltpu.SemaphoreType.DMA((2,)),
                 pltpu.SemaphoreType.REGULAR,
             ],
             compiler_params=pltpu.CompilerParams(collective_id=0, has_side_effects=True, vmem_limit_bytes=43 * 2 ** 20),
         )(w_in, jnp.transpose(w_out), jnp.transpose(obs_op),
           jnp.transpose(obs_val, (0, 1, 3, 2)), jnp.transpose(obs_wt, (0, 1, 3, 2)), state)
+        tail_a = lax.ppermute(tail_a, 'ens', [(i, (i + 2) % OWNERS) for i in range(OWNERS)])
+        tail_b = lax.ppermute(tail_b, 'ens', [(i, OWNERS - 1 - i) for i in range(OWNERS)])
         result = pl.pallas_call(
             store_kernel,
             out_shape=jax.ShapeDtypeStruct(state.shape, BF16),
@@ -527,7 +581,17 @@
             out_specs=hbm,
             scratch_shapes=[pltpu.SemaphoreType.DMA((STORES,))],
             compiler_params=pltpu.CompilerParams(vmem_limit_bytes=2 ** 20),
+            cost_estimate=pl.CostEstimate(flops=0, bytes_accessed=2 * state.size, transcendentals=0),
         )(pltpu.with_memory_space_constraint(held, pltpu.VMEM))
+        result = pl.pallas_call(
+            join_kernel,
+            out_shape=jax.ShapeDtypeStruct(state.shape, BF16),
+            in_specs=[hbm, vmem, vmem],
+            out_specs=hbm,
+            scratch_shapes=[pltpu.SemaphoreType.DMA((2,))],
+            input_output_aliases={0: 0},
+            compiler_params=pltpu.CompilerParams(vmem_limit_bytes=2 ** 20),
+        )(result, tail_a, tail_b)
         return jnp.transpose(result, (0, 1, 3, 2))
 
     state_spec = P('ens', 'lat', 'dom', None)

time: 373 us -> 371 us (level)
  Pallas kernels: 373 us -> 368 us
    pallas_call x1, Pallas kernels: 367 us -> 362 us  [local_cycle(): pl.pallas_call(functools.partial(kernel, lat_count, dom_count), out_shape...]
  transfers between devices with their start and end apart: 0 -> 2, of which waited for: 0 -> 1; matrix products, arithmetic and copies ran while one was open for 0% -> 0% of each run, Pallas kernels for 0% -> 2%
where the time goes in v7:
time: 371 us
  Pallas kernels  368 us (99%)
    pallas_call x1, Pallas kernels, local_cycle(): pl.pallas_call(functools.partial(kernel, lat_count, dom_count), out_shape...  362 us
  transfers between devices with their start and end apart: 2, of which 1 were waited for; matrix products, arithmetic and copies ran while one was open for 0% of the time, Pallas kernels for 2%

profile of v7, /device:TPU:0, one launch (start us, length us, event | category | flops | bytes accessed | tf_op | source)
XLA Modules:
  0.0 370.8 jit_solution(9607816177211038581)
XLA Ops:
  0.0 361.5 %shard_map.64 = (bf16[64,10,32,512]{3,2,1,0:T(8,128)(2,1)S(1)}, bf16[8,32,256]{2,1,0:T(8,128)(2,1)}, bf16[8,32,256]{2,1,0:T(8,128)(2,1)}) custom-call(bf16[64,128]{1,0:T(8,128)(2,1)} %w_in_hbm.1, bf16[32,128]{1,0:T(8,128)(2,1)} %bitcast.9, bf16[16,32]{1,0:T(8,128)(2,1)} %bitcast.10, f32[8,2,16,256]{3,2,1,0:T(8,128)} %bitcast.7, f32[8,2,16,256]{3,2,1,0:T(8,128)} %bitcast.8, ...), custom_call_target="tpu_custom_call" | custom-call | tf_op jit(solution)/shard_map/pallas_call | solution.py:524
  361.5 0.6 collective-permute-start
  362.1 1.5 collective-permute-start.1
  363.6 5.9 %shard_map.65.whole = bf16[64,8,32,512]{3,2,1,0:T(8,128)(2,1)} custom-call(bf16[64,10,32,512]{3,2,1,0:T(8,128)(2,1)S(1)} %get-tuple-element.8.held), custom_call_target="tpu_custom_call" | custom-call | bytes 16777216 | tf_op jit(solution)/shard_map/pallas_call | solution.py:577
  369.5 0.0 collective-permute-done.piece_a
  369.5 0.6 collective-permute-done.1.piece_b
  370.1 0.7 shard_map.66
Async XLA Ops:
  361.5 8.0 %collective-permute-start = (bf16[8,32,256]{2,1,0:T(8,128)(2,1)}, bf16[8,32,256]{2,1,0:T(8,128)(2,1)S(1)}, u32[]{:S(2)}, u32[]{:S(2)}) collective-permute-start(bf16[8,32,256]{2,1,0:T(8,128)(2,1)} %get-tuple-element.9), channel_id=1, source_target_pairs={{0,2},{1,3},{2,0},{3,1},{4,6},{5,7},{6,4},{7,5},{8,10},{9,11},{10,... | collective-permute-start | bytes 393224 | tf_op jit(solution)/shard_map/ppermute | solution.py:575
  362.1 8.0 %collective-permute-start.1 = (bf16[8,32,256]{2,1,0:T(8,128)(2,1)}, bf16[8,32,256]{2,1,0:T(8,128)(2,1)S(1)}, u32[]{:S(2)}, u32[]{:S(2)}) collective-permute-start(bf16[8,32,256]{2,1,0:T(8,128)(2,1)} %get-tuple-element.10), channel_id=1, source_target_pairs={{0,3},{1,2},{2,1},{3,0},{4,7},{5,6},{6,5},{7,4},{8,11},{9,10},{10,... | collective-permute-start | bytes 393224 | tf_op jit(solution)/shard_map/ppermute | solution.py:576

commit v8 on v7

--- a/solution.py
+++ b/solution.py
@@ -25,7 +25,7 @@
 BATCH = 4
 PACK = 8
 STORES = 8
-TAIL = 8
+TAIL = 10
 MAIN = MINE - TAIL
 SUBS = MINE // GROUP
 FIRST = 16
@@ -61,7 +61,7 @@
 
 def kernel(lat_count, dom_count, w_in_hbm, w_out_hbm, op_hbm, yo_hbm, wt_hbm, x_ref, xbuf, tail_a, tail_b,
            buf, w_in_ref, w2_ref, op_ref, w1_ref, bd_ref, perm_ref, yo_ref, wt_ref, edge_out, edge_in, work, am, pm, zm, cif, sy, sz, st, xbar, ybar, sw_ref, sd_ref,
-           first_sem, upper_sem, lower_sem, small_sem, halo_send, halo_recv, halo_local, edge_send, edge_recv, f_send, f_recv, r_send, r_recv, last_send, last_recv, tail_sem, obs_sem, ready):
+           first_sem, upper_sem, lower_sem, small_sem, halo_send, halo_recv, halo_local, edge_send, edge_recv, f_send, f_recv, r_send, r_recv, last_send, last_recv, obs_sem, ready):
     me = lax.axis_index('ens')
     lat = lax.axis_index('lat')
     dom = lax.axis_index('dom')
@@ -309,10 +309,6 @@
             last_send.at[chunk, t - 1], last_recv.at[chunk, source],
             device_id={'ens': (me + t) % OWNERS}, device_id_type=MESH)
 
-    def tail_copy(chunk, t):
-        source = buf.at[STAGE + 3 * chunk + t - 1, MAIN:MINE]
-        return pltpu.make_async_copy(source, tail_a if t == 2 else tail_b, tail_sem.at[0 if t == 2 else 1])
-
     def leaves(chunk, t):
         crosses = {1: me % 2, 2: 1, 3: 1 - me % 2}[t]
         return (chunk // (CHUNKS - 1)) * crosses == 1
@@ -445,15 +441,16 @@
                         xbuf[pl.ds(index * GROUP, GROUP), own_row, part * 16:part * 16 + 16, own_span] = moved
                     else:
                         buf[STAGE + 3 * chunk + t - 1, pl.ds(index * GROUP, GROUP), part * 16:part * 16 + 16] = moved
+
+                        @pl.when((index == SUBS - 1) & leaves(chunk, t))
+                        def _():
+                            tail_ref = tail_a if t == 2 else tail_b
+                            tail_ref[:, part * 16:part * 16 + 16] = moved[GROUP - TAIL:]
                 return carry
 
             lax.fori_loop(0, SUBS, by_member, 0)
             if t:
                 r_copy(chunk, t, me).start()
-
-                @pl.when(leaves(chunk, t))
-                def _():
-                    tail_copy(chunk, t).start()
 
                 @pl.when(jnp.logical_not(leaves(chunk, t)))
                 def _():
@@ -466,10 +463,6 @@
         for t in range(1, OWNERS):
             r_copy(chunk, t, (me + t) % OWNERS).wait_recv()
             r_copy(chunk, t, me).wait_send()
-
-            @pl.when(leaves(chunk, t))
-            def _():
-                tail_copy(chunk, t).wait()
 
             @pl.when(jnp.logical_not(leaves(chunk, t)))
             def _():
@@ -520,12 +513,12 @@
         state = jnp.transpose(ens_block, (0, 1, 3, 2))
         vmem = pl.BlockSpec(memory_space=pltpu.VMEM)
         hbm = pl.BlockSpec(memory_space=pl.ANY)
-        tail = jax.ShapeDtypeStruct((TAIL, CHANS, PATCH), BF16)
+        tail = pltpu.VMEM((TAIL, CHANS, PATCH), BF16)
         held, tail_a, tail_b = pl.pallas_call(
             functools.partial(kernel, lat_count, dom_count),
             out_shape=(pltpu.VMEM((MINE, ROWS + 2, CHANS, COLS), BF16), tail, tail),
             in_specs=[hbm] * 6,
-            out_specs=(vmem, hbm, hbm),
+            out_specs=(vmem, vmem, vmem),
             scratch_shapes=[
                 pltpu.VMEM((STAGE + 3 * CHUNKS, MINE, CHANS, PATCH), BF16),
                 pltpu.VMEM((2 * CHANS, 128), BF16),
@@ -566,7 +559,6 @@
                 pltpu.SemaphoreType.DMA((CHUNKS, 3)),
                 pltpu.SemaphoreType.DMA((CHUNKS, OWNERS)),
                 pltpu.SemaphoreType.DMA((2,)),
-                pltpu.SemaphoreType.DMA((2,)),
                 pltpu.SemaphoreType.REGULAR,
             ],
             compiler_params=pltpu.CompilerParams(collective_id=0, has_side_effects=True, vmem_limit_bytes=43 * 2 ** 20),

time: 371 us -> 371 us (level)
  no operation moved by 1% of the time
where the time goes in v8:
time: 371 us
  Pallas kernels  367 us (99%)
    pallas_call x1, Pallas kernels, local_cycle(): pl.pallas_call(functools.partial(kernel, lat_count, dom_count), out_shape...  360 us
  transfers between devices with their start and end apart: 2, of which 1 were waited for; matrix products, arithmetic and copies ran while one was open for 0% of the time, Pallas kernels for 2%

profile of v8, /device:TPU:0, one launch (start us, length us, event | category | flops | bytes accessed | tf_op | source)
XLA Modules:
  0.0 370.8 jit_solution(14677600890902363151)
XLA Ops:
  0.0 360.1 %shard_map.64 = (bf16[64,10,32,512]{3,2,1,0:T(8,128)(2,1)S(1)}, bf16[10,32,256]{2,1,0:T(8,128)(2,1)S(1)}, bf16[10,32,256]{2,1,0:T(8,128)(2,1)S(1)}) custom-call(bf16[64,128]{1,0:T(8,128)(2,1)} %w_in_hbm.1, bf16[32,128]{1,0:T(8,128)(2,1)} %bitcast.9, bf16[16,32]{1,0:T(8,128)(2,1)} %bitcast.10, f32[8,2,16,256]{3,2,1,0:T(8,128)} %bitcast.7, ...), custom_call_target="tpu_custom_call" | custom-call | tf_op jit(solution)/shard_map/pallas_call | solution.py:517
  360.1 0.6 collective-permute-start
  360.7 1.4 collective-permute-start.1
  362.2 5.9 %shard_map.65.whole = bf16[64,8,32,512]{3,2,1,0:T(8,128)(2,1)} custom-call(bf16[64,10,32,512]{3,2,1,0:T(8,128)(2,1)S(1)} %get-tuple-element.8.held), custom_call_target="tpu_custom_call" | custom-call | bytes 16777216 | tf_op jit(solution)/shard_map/pallas_call | solution.py:569
  368.1 0.0 collective-permute-done.piece_a
  368.1 2.0 collective-permute-done.1.piece_b
  370.1 0.7 shard_map.66
Async XLA Ops:
  360.1 8.0 %collective-permute-start = (bf16[10,32,256]{2,1,0:T(8,128)(2,1)S(1)}, bf16[10,32,256]{2,1,0:T(8,128)(2,1)S(1)}, u32[]{:S(2)}, u32[]{:S(2)}) collective-permute-start(bf16[10,32,256]{2,1,0:T(8,128)(2,1)S(1)} %get-tuple-element.9), channel_id=1, source_target_pairs={{0,2},{1,3},{2,0},{3,1},{4,6},{5,7},{6,4},{7,5},{8,10},{9,11},{10,... | collective-permute-start | bytes 491528 | tf_op jit(solution)/shard_map/ppermute | solution.py:567
  360.7 9.4 %collective-permute-start.1 = (bf16[10,32,256]{2,1,0:T(8,128)(2,1)S(1)}, bf16[10,32,256]{2,1,0:T(8,128)(2,1)S(1)}, u32[]{:S(2)}, u32[]{:S(2)}) collective-permute-start(bf16[10,32,256]{2,1,0:T(8,128)(2,1)S(1)} %get-tuple-element.10), channel_id=1, source_target_pairs={{0,3},{1,2},{2,1},{3,0},{4,7},{5,6},{6,5},{7,4},{8,11},{9,10},{10,... | collective-permute-start | bytes 491528 | tf_op jit(solution)/shard_map/ppermute | solution.py:568

commit v9 on v8

--- a/solution.py
+++ b/solution.py
@@ -25,8 +25,9 @@
 BATCH = 4
 PACK = 8
 STORES = 8
-TAIL = 10
+TAIL = 16
 MAIN = MINE - TAIL
+LAST_CHUNK = {1: CHUNKS, 2: CHUNKS - 1, 3: CHUNKS}
 SUBS = MINE // GROUP
 FIRST = 16
 INNER = 32
@@ -59,7 +60,7 @@
     return (1 - last) * (1 + 2 * chunk + which) + last * (ROWS - 1) * which
 
 
-def kernel(lat_count, dom_count, w_in_hbm, w_out_hbm, op_hbm, yo_hbm, wt_hbm, x_ref, xbuf, tail_a, tail_b,
+def kernel(lat_count, dom_count, w_in_hbm, w_out_hbm, op_hbm, yo_hbm, wt_hbm, x_ref, xbuf, tail_ref,
            buf, w_in_ref, w2_ref, op_ref, w1_ref, bd_ref, perm_ref, yo_ref, wt_ref, edge_out, edge_in, work, am, pm, zm, cif, sy, sz, st, xbar, ybar, sw_ref, sd_ref,
            first_sem, upper_sem, lower_sem, small_sem, halo_send, halo_recv, halo_local, edge_send, edge_recv, f_send, f_recv, r_send, r_recv, last_send, last_recv, obs_sem, ready):
     me = lax.axis_index('ens')
@@ -309,10 +310,6 @@
             last_send.at[chunk, t - 1], last_recv.at[chunk, source],
             device_id={'ens': (me + t) % OWNERS}, device_id_type=MESH)
 
-    def leaves(chunk, t):
-        crosses = {1: me % 2, 2: 1, 3: 1 - me % 2}[t]
-        return (chunk // (CHUNKS - 1)) * crosses == 1
-
     def analyse(chunk, carry):
         for t in range(1, OWNERS):
             source = (me + t) % OWNERS
@@ -442,17 +439,17 @@
                     else:
                         buf[STAGE + 3 * chunk + t - 1, pl.ds(index * GROUP, GROUP), part * 16:part * 16 + 16] = moved
 
-                        @pl.when((index == SUBS - 1) & leaves(chunk, t))
-                        def _():
-                            tail_ref = tail_a if t == 2 else tail_b
-                            tail_ref[:, part * 16:part * 16 + 16] = moved[GROUP - TAIL:]
+                        if t == 2:
+                            @pl.when((index == SUBS - 1) & (chunk == CHUNKS - 1))
+                            def _():
+                                tail_ref[:, part * 16:part * 16 + 16] = moved
                 return carry
 
             lax.fori_loop(0, SUBS, by_member, 0)
             if t:
                 r_copy(chunk, t, me).start()
 
-                @pl.when(jnp.logical_not(leaves(chunk, t)))
+                @pl.when(chunk < LAST_CHUNK[t])
                 def _():
                     last_copy(chunk, t, me).start()
         return carry
@@ -464,7 +461,7 @@
             r_copy(chunk, t, (me + t) % OWNERS).wait_recv()
             r_copy(chunk, t, me).wait_send()
 
-            @pl.when(jnp.logical_not(leaves(chunk, t)))
+            @pl.when(chunk < LAST_CHUNK[t])
             def _():
                 last_copy(chunk, t, (me + t) % OWNERS).wait_recv()
                 last_copy(chunk, t, me).wait_send()
@@ -492,17 +489,12 @@
         copy.wait()
 
 
-def join_kernel(whole, piece_a, piece_b, out_ref, sems):
-    me = lax.axis_index('ens')
-    copies = []
-    for index, (piece, source) in enumerate(((piece_a, (me + 2) % OWNERS), (piece_b, OWNERS - 1 - me))):
-        span = pl.ds(pl.multiple_of((source % 2) * PATCH, PATCH), PATCH)
-        row = chunk_row(CHUNKS - 1, source // 2)
-        copies.append(pltpu.make_async_copy(piece, out_ref.at[MAIN:MINE, row, :, span], sems.at[index]))
-    for copy in copies:
-        copy.start()
-    for copy in copies:
-        copy.wait()
+def join_kernel(whole, piece, out_ref, sem):
+    source = (lax.axis_index('ens') + 2) % OWNERS
+    span = pl.ds(pl.multiple_of((source % 2) * PATCH, PATCH), PATCH)
+    copy = pltpu.make_async_copy(piece, out_ref.at[MAIN:MINE, chunk_row(CHUNKS - 1, source // 2), :, span], sem)
+    copy.start()
+    copy.wait()
 
 
 def solution(mesh):
@@ -514,11 +506,11 @@
         vmem = pl.BlockSpec(memory_space=pltpu.VMEM)
         hbm = pl.BlockSpec(memory_space=pl.ANY)
         tail = pltpu.VMEM((TAIL, CHANS, PATCH), BF16)
-        held, tail_a, tail_b = pl.pallas_call(
+        held, tail_piece = pl.pallas_call(
             functools.partial(kernel, lat_count, dom_count),
-            out_shape=(pltpu.VMEM((MINE, ROWS + 2, CHANS, COLS), BF16), tail, tail),
+            out_shape=(pltpu.VMEM((MINE, ROWS + 2, CHANS, COLS), BF16), tail),
             in_specs=[hbm] * 6,
-            out_specs=(vmem, vmem, vmem),
+            out_specs=(vmem, vmem),
             scratch_shapes=[
                 pltpu.VMEM((STAGE + 3 * CHUNKS, MINE, CHANS, PATCH), BF16),
                 pltpu.VMEM((2 * CHANS, 128), BF16),
@@ -564,8 +556,7 @@
             compiler_params=pltpu.CompilerParams(collective_id=0, has_side_effects=True, vmem_limit_bytes=43 * 2 ** 20),
         )(w_in, jnp.transpose(w_out), jnp.transpose(obs_op),
           jnp.transpose(obs_val, (0, 1, 3, 2)), jnp.transpose(obs_wt, (0, 1, 3, 2)), state)
-        tail_a = lax.ppermute(tail_a, 'ens', [(i, (i + 2) % OWNERS) for i in range(OWNERS)])
-        tail_b = lax.ppermute(tail_b, 'ens', [(i, OWNERS - 1 - i) for i in range(OWNERS)])
+        tail_piece = lax.ppermute(tail_piece, 'ens', [(i, (i + 2) % OWNERS) for i in range(OWNERS)])
         result = pl.pallas_call(
             store_kernel,
             out_shape=jax.ShapeDtypeStruct(state.shape, BF16),
@@ -578,12 +569,12 @@
         result = pl.pallas_call(
             join_kernel,
             out_shape=jax.ShapeDtypeStruct(state.shape, BF16),
-            in_specs=[hbm, vmem, vmem],
+            in_specs=[hbm, vmem],
             out_specs=hbm,
-            scratch_shapes=[pltpu.SemaphoreType.DMA((2,))],
+            scratch_shapes=[pltpu.SemaphoreType.DMA],
             input_output_aliases={0: 0},
             compiler_params=pltpu.CompilerParams(vmem_limit_bytes=2 ** 20),
-        )(result, tail_a, tail_b)
+        )(result, tail_piece)
         return jnp.transpose(result, (0, 1, 3, 2))
 
     state_spec = P('ens', 'lat', 'dom', None)

time: 371 us -> 371 us (level)
  transfers between devices with their start and end apart: 2 -> 1, of which waited for: 1 -> 1; matrix products, arithmetic and copies ran while one was open for 0% -> 0% of each run, Pallas kernels for 2% -> 2%
where the time goes in v9:
time: 371 us
  Pallas kernels  368 us (99%)
    pallas_call x1, Pallas kernels, local_cycle(): pl.pallas_call(functools.partial(kernel, lat_count, dom_count), out_shape...  362 us
  transfers between devices with their start and end apart: 1, of which 1 were waited for; matrix products, arithmetic and copies ran while one was open for 0% of the time, Pallas kernels for 2%

profile of v9, /device:TPU:0, one launch (start us, length us, event | category | flops | bytes accessed | tf_op | source)
XLA Modules:
  0.0 371.1 jit_solution(15994478712601163704)
XLA Ops:
  0.0 361.5 %shard_map.64 = (bf16[64,10,32,512]{3,2,1,0:T(8,128)(2,1)S(1)}, bf16[16,32,256]{2,1,0:T(8,128)(2,1)S(1)}) custom-call(bf16[64,128]{1,0:T(8,128)(2,1)} %w_in_hbm.1, bf16[32,128]{1,0:T(8,128)(2,1)} %bitcast.9, bf16[16,32]{1,0:T(8,128)(2,1)} %bitcast.10, f32[8,2,16,256]{3,2,1,0:T(8,128)} %bitcast.7, f32[8,2,16,256]{3,2,1,0:T(8,128)} %bitcast.8, ...), custom_call_target="tpu_custom_call" | custom-call | tf_op jit(solution)/shard_map/pallas_call | solution.py:509
  361.5 0.6 collective-permute-start
  362.1 5.9 %shard_map.65.whole = bf16[64,8,32,512]{3,2,1,0:T(8,128)(2,1)} custom-call(bf16[64,10,32,512]{3,2,1,0:T(8,128)(2,1)S(1)} %get-tuple-element.7.held), custom_call_target="tpu_custom_call" | custom-call | bytes 16777216 | tf_op jit(solution)/shard_map/pallas_call | solution.py:560
  368.0 2.4 collective-permute-done.piece
  370.4 0.7 shard_map.66
Async XLA Ops:
  361.5 8.9 %collective-permute-start = (bf16[16,32,256]{2,1,0:T(8,128)(2,1)S(1)}, bf16[16,32,256]{2,1,0:T(8,128)(2,1)S(1)}, u32[]{:S(2)}, u32[]{:S(2)}) collective-permute-start(bf16[16,32,256]{2,1,0:T(8,128)(2,1)S(1)} %get-tuple-element.8), channel_id=1, source_target_pairs={{0,2},{1,3},{2,0},{3,1},{4,6},{5,7},{6,4},{7,5},{8,10},{9,11},{10,... | collective-permute-start | bytes 786440 | tf_op jit(solution)/shard_map/ppermute | solution.py:559

commit v10 on v8

--- a/solution.py
+++ b/solution.py
@@ -198,15 +198,18 @@
         for t in (2, 1, 3):
             f_copy(chunk, t, start, size, kind).start()
 
-    def forecast(chunk, start, stop, kind):
+    def forecast(chunk, start, stop, kind, whole=False):
         def step(index, carry):
             if kind == 'inner' and start == BATCH:
                 first_copy(index).wait()
             members(chunk, index * BATCH, BATCH, kind)
-            send(chunk, index * BATCH, BATCH, kind)
+            if not whole:
+                send(chunk, index * BATCH, BATCH, kind)
             return carry
 
         lax.fori_loop(start // BATCH, stop // BATCH, step, 0)
+        if whole:
+            send(chunk, start, stop - start, kind)
 
     first_copy(0).wait()
     members(0, 0, BATCH // 2, 'inner')
@@ -272,7 +275,7 @@
         def _():
             pack(chunk + 1)
 
-        forecast(chunk, 0, MINE, 'all')
+        forecast(chunk, 0, MINE, 'all', whole=True)
         return carry
 
     lax.fori_loop(1, CHUNKS, forecast_chunk, 0)

time: 371 us -> 371 us (level)
  no operation moved by 1% of the time
where the time goes in v10:
time: 371 us
  Pallas kernels  367 us (99%)
    pallas_call x1, Pallas kernels, local_cycle(): pl.pallas_call(functools.partial(kernel, lat_count, dom_count), out_shape...  360 us
  transfers between devices with their start and end apart: 2, of which 1 were waited for; matrix products, arithmetic and copies ran while one was open for 0% of the time, Pallas kernels for 2%

profile of v10, /device:TPU:0, one launch (start us, length us, event | category | flops | bytes accessed | tf_op | source)
XLA Modules:
  0.0 370.8 jit_solution(6966370751004516200)
XLA Ops:
  0.0 360.1 %shard_map.64 = (bf16[64,10,32,512]{3,2,1,0:T(8,128)(2,1)S(1)}, bf16[10,32,256]{2,1,0:T(8,128)(2,1)S(1)}, bf16[10,32,256]{2,1,0:T(8,128)(2,1)S(1)}) custom-call(bf16[64,128]{1,0:T(8,128)(2,1)} %w_in_hbm.1, bf16[32,128]{1,0:T(8,128)(2,1)} %bitcast.9, bf16[16,32]{1,0:T(8,128)(2,1)} %bitcast.10, f32[8,2,16,256]{3,2,1,0:T(8,128)} %bitcast.7, ...), custom_call_target="tpu_custom_call" | custom-call | tf_op jit(solution)/shard_map/pallas_call | solution.py:520
  360.1 0.6 collective-permute-start
  360.7 1.5 collective-permute-start.1
  362.2 5.9 %shard_map.65.whole = bf16[64,8,32,512]{3,2,1,0:T(8,128)(2,1)} custom-call(bf16[64,10,32,512]{3,2,1,0:T(8,128)(2,1)S(1)} %get-tuple-element.8.held), custom_call_target="tpu_custom_call" | custom-call | bytes 16777216 | tf_op jit(solution)/shard_map/pallas_call | solution.py:572
  368.1 0.0 collective-permute-done.piece_a
  368.1 2.0 collective-permute-done.1.piece_b
  370.1 0.7 shard_map.66
Async XLA Ops:
  360.1 8.0 %collective-permute-start = (bf16[10,32,256]{2,1,0:T(8,128)(2,1)S(1)}, bf16[10,32,256]{2,1,0:T(8,128)(2,1)S(1)}, u32[]{:S(2)}, u32[]{:S(2)}) collective-permute-start(bf16[10,32,256]{2,1,0:T(8,128)(2,1)S(1)} %get-tuple-element.9), channel_id=1, source_target_pairs={{0,2},{1,3},{2,0},{3,1},{4,6},{5,7},{6,4},{7,5},{8,10},{9,11},{10,... | collective-permute-start | bytes 491528 | tf_op jit(solution)/shard_map/ppermute | solution.py:570
  360.7 9.4 %collective-permute-start.1 = (bf16[10,32,256]{2,1,0:T(8,128)(2,1)S(1)}, bf16[10,32,256]{2,1,0:T(8,128)(2,1)S(1)}, u32[]{:S(2)}, u32[]{:S(2)}) collective-permute-start(bf16[10,32,256]{2,1,0:T(8,128)(2,1)S(1)} %get-tuple-element.10), channel_id=1, source_target_pairs={{0,3},{1,2},{2,1},{3,0},{4,7},{5,6},{6,5},{7,4},{8,11},{9,10},{10,... | collective-permute-start | bytes 491528 | tf_op jit(solution)/shard_map/ppermute | solution.py:571
